TPU v7x, 32 devices: a whole 2x2x4 slice. The times are simulated.
32 devices in a mesh: replica: 4 (over y, core), model: 8 (over z, x).
Axes of the slice: x: 2, y: 2, z: 4, core: 2. Of those that a mesh axis runs over, the one named last changes fastest.
Arguments:
- partial_query: float32 [4, 2048, 2048], P('replica', None, 'model'), may hold values from -4 to 4
- partial_key: float32 [4, 2048, 2048], P('replica', None, 'model'), may hold values from -4 to 4
- partial_value: float32 [4, 2048, 2048], P('replica', None, 'model'), may hold values from -4 to 4
- partial_mixed: float32 [4, 2048, 2048], P('replica', 'model'), may hold values from -4 to 4
- partial_norm: float32 [4, 2048], P('replica'), may hold values from -8 to 8
- partial_bias: float32 [4, 2048], P('replica'), may hold values from -8 to 8
- master_query: float32 [2048, 2048], P('replica', 'model'), may hold values from -0.1875 to 0.1875
- master_key: float32 [2048, 2048], P('replica', 'model'), may hold values from -0.1875 to 0.1875
- master_value: float32 [2048, 2048], P('replica', 'model'), may hold values from -0.1875 to 0.1875
- master_mixed: float32 [2048, 2048], P('model', 'replica'), may hold values from -0.1875 to 0.1875
- master_norm: float32 [2048], P('replica'), may hold values from 0.25 to 1.75
- master_bias: float32 [2048], P('replica'), may hold values from -3 to 3
- memory_query: float32 [2048, 2048], P('replica', 'model'), may hold values from 9.765625e-05 to 0.0009765625
- memory_key: float32 [2048, 2048], P('replica', 'model'), may hold values from 9.765625e-05 to 0.0009765625
- memory_value: float32 [2048, 2048], P('replica', 'model'), may hold values from 9.765625e-05 to 0.0009765625
- memory_mixed: float32 [2048, 2048], P('model', 'replica'), may hold values from 9.765625e-05 to 0.0009765625
- memory_norm: float32 [2048], P('replica'), may hold values from 0.05 to 0.8
- memory_bias: float32 [2048], P('replica'), may hold values from 0.05 to 0.8
Outputs:
- compute_query: bfloat16 [2048, 2048], P(None, 'model')
- compute_key: bfloat16 [2048, 2048], P(None, 'model')
- compute_value: bfloat16 [2048, 2048], P(None, 'model')
- compute_mixed: bfloat16 [2048, 2048], P('model')
- compute_norm: bfloat16 [2048], replicated
- compute_bias: bfloat16 [2048], replicated
- stepped_query: float32 [2048, 2048], P('replica', 'model')
- stepped_key: float32 [2048, 2048], P('replica', 'model')
- stepped_value: float32 [2048, 2048], P('replica', 'model')
- stepped_mixed: float32 [2048, 2048], P('model', 'replica')
- stepped_norm: float32 [2048], P('replica')
- stepped_bias: float32 [2048], P('replica')
- state_new_query: float32 [2048, 2048], P('replica', 'model')
- state_new_key: float32 [2048, 2048], P('replica', 'model')
- state_new_value: float32 [2048, 2048], P('replica', 'model')
- state_new_mixed: float32 [2048, 2048], P('model', 'replica')
- state_new_norm: float32 [2048], P('replica')
- state_new_bias: float32 [2048], P('replica')
All inputs are finite; a program needn't handle non-finite values.
Results may differ from a plain program's by a relative error of at most 0.0004.
Values may be sent and summed in bfloat16 or wider, within the bound.
No kernel may reach another device: no remote copies, remote signals or barrier semaphores. Data moves between devices by JAX's collectives and lax.ppermute only.
A program may use at most 64 MiB of HBM per device.

v0:
```python
import jax
import jax.numpy as jnp
from jax import lax
from jax.sharding import PartitionSpec as P

learn_rate = 0.015
hold_rate = 0.8


def shards(
    partial_query,
    partial_key,
    partial_value,
    partial_mixed,
    partial_norm,
    partial_bias,
    master_query,
    master_key,
    master_value,
    master_mixed,
    master_norm,
    master_bias,
    memory_query,
    memory_key,
    memory_value,
    memory_mixed,
    memory_norm,
    memory_bias,
):
    mean_query, mean_key, mean_value, mean_mixed = (
        lax.psum_scatter(partial_query[0], "replica", scatter_dimension=0, tiled=True),
        lax.psum_scatter(partial_key[0], "replica", scatter_dimension=0, tiled=True),
        lax.psum_scatter(partial_value[0], "replica", scatter_dimension=0, tiled=True),
        lax.psum_scatter(partial_mixed[0], "replica", scatter_dimension=1, tiled=True),
    )
    whole_norm, whole_bias = lax.psum((partial_norm[0], partial_bias[0]), "replica")
    place = lax.axis_index("replica")
    mean_norm = lax.dynamic_slice_in_dim(
        whole_norm, place * master_norm.shape[0], master_norm.shape[0]
    )
    mean_bias = lax.dynamic_slice_in_dim(
        whole_bias, place * master_bias.shape[0], master_bias.shape[0]
    )
    mean_rate = lax.axis_size("replica") ** (-0.5)
    mean_query = mean_query * mean_rate
    mean_key = mean_key * mean_rate
    mean_value = mean_value * mean_rate
    mean_mixed = mean_mixed * mean_rate
    mean_norm = mean_norm * mean_rate
    mean_bias = mean_bias * mean_rate
    (
        own_query,
        own_key,
        own_value,
        own_mixed,
        slope_query_norm,
        slope_key_norm,
        slope_value_norm,
        slope_mixed_norm,
    ) = lax.psum(
        (
            jnp.sum(master_query * master_query, axis=1, keepdims=True),
            jnp.sum(master_key * master_key, axis=1, keepdims=True),
            jnp.sum(master_value * master_value, axis=1, keepdims=True),
            jnp.sum(master_mixed * master_mixed, axis=0, keepdims=True),
            jnp.sum(mean_query * mean_query, axis=1, keepdims=True),
            jnp.sum(mean_key * mean_key, axis=1, keepdims=True),
            jnp.sum(mean_value * mean_value, axis=1, keepdims=True),
            jnp.sum(mean_mixed * mean_mixed, axis=0, keepdims=True),
        ),
        "model",
    )
    mean_query = mean_query * (jnp.sqrt(own_query) * lax.rsqrt(slope_query_norm + 1e-06))
    mean_key = mean_key * (jnp.sqrt(own_key) * lax.rsqrt(slope_key_norm + 1e-06))
    mean_value = mean_value * (jnp.sqrt(own_value) * lax.rsqrt(slope_value_norm + 1e-06))
    mean_mixed = mean_mixed * (jnp.sqrt(own_mixed) * lax.rsqrt(slope_mixed_norm + 1e-06))
    state_new_query = hold_rate * memory_query + (1.0 - hold_rate) * mean_query * mean_query
    stepped_query = master_query - learn_rate * mean_query * lax.rsqrt(state_new_query + 1e-06)
    state_new_key = hold_rate * memory_key + (1.0 - hold_rate) * mean_key * mean_key
    stepped_key = master_key - learn_rate * mean_key * lax.rsqrt(state_new_key + 1e-06)
    state_new_value = hold_rate * memory_value + (1.0 - hold_rate) * mean_value * mean_value
    stepped_value = master_value - learn_rate * mean_value * lax.rsqrt(state_new_value + 1e-06)
    state_new_mixed = hold_rate * memory_mixed + (1.0 - hold_rate) * mean_mixed * mean_mixed
    stepped_mixed = master_mixed - learn_rate * mean_mixed * lax.rsqrt(state_new_mixed + 1e-06)
    state_new_norm = hold_rate * memory_norm + (1.0 - hold_rate) * mean_norm * mean_norm
    stepped_norm = master_norm - learn_rate * mean_norm * lax.rsqrt(state_new_norm + 1e-06)
    state_new_bias = hold_rate * memory_bias + (1.0 - hold_rate) * mean_bias * mean_bias
    stepped_bias = master_bias - learn_rate * mean_bias * lax.rsqrt(state_new_bias + 1e-06)
    compute_query, compute_key, compute_value, compute_mixed, compute_norm, compute_bias = (
        lax.all_gather(stepped_query.astype(jnp.bfloat16), "replica", axis=0, tiled=True),
        lax.all_gather(stepped_key.astype(jnp.bfloat16), "replica", axis=0, tiled=True),
        lax.all_gather(stepped_value.astype(jnp.bfloat16), "replica", axis=0, tiled=True),
        lax.all_gather(stepped_mixed.astype(jnp.bfloat16), "replica", axis=1, tiled=True),
        lax.all_gather(stepped_norm.astype(jnp.bfloat16), "replica", axis=0, tiled=True),
        lax.all_gather(stepped_bias.astype(jnp.bfloat16), "replica", axis=0, tiled=True),
    )
    return (
        compute_query,
        compute_key,
        compute_value,
        compute_mixed,
        compute_norm,
        compute_bias,
        stepped_query,
        stepped_key,
        stepped_value,
        stepped_mixed,
        stepped_norm,
        stepped_bias,
        state_new_query,
        state_new_key,
        state_new_value,
        state_new_mixed,
        state_new_norm,
        state_new_bias,
    )


def solution(mesh):
    in_specs = (
        P("replica", None, "model"),
        P("replica", None, "model"),
        P("replica", None, "model"),
        P("replica", "model", None),
        P("replica", None),
        P("replica", None),
        P("replica", "model"),
        P("replica", "model"),
        P("replica", "model"),
        P("model", "replica"),
        P("replica"),
        P("replica"),
        P("replica", "model"),
        P("replica", "model"),
        P("replica", "model"),
        P("model", "replica"),
        P("replica"),
        P("replica"),
    )
    out_specs = (
        P(None, "model"),
        P(None, "model"),
        P(None, "model"),
        P("model", None),
        P(),
        P(),
        P("replica", "model"),
        P("replica", "model"),
        P("replica", "model"),
        P("model", "replica"),
        P("replica"),
        P("replica"),
        P("replica", "model"),
        P("replica", "model"),
        P("replica", "model"),
        P("model", "replica"),
        P("replica"),
        P("replica"),
    )
    return jax.shard_map(shards, mesh=mesh, in_specs=in_specs, out_specs=out_specs, check_vma=False)
```

profile of v0, /device:TPU:0, one launch (start us, length us, event | category | flops | bytes accessed | tf_op | source)
XLA Modules:
  0.0 268.1 jit_solution(13964327610522615378)
XLA Ops:
  7.2 0.0 reduce-scatter.9.cloned.1.call-start
  7.2 0.7 reduce-scatter.9.cloned.1.call-update
  7.9 0.0 reduce-scatter.11.cloned.1.call-start
  8.0 0.7 reduce-scatter.11.cloned.1.call-update
  8.7 0.0 reduce-scatter.5.cloned.1.call-start
  8.7 0.7 reduce-scatter.5.cloned.1.call-update
  9.4 0.0 reduce-scatter.7.cloned.1.call-start
  9.5 0.5 reduce-scatter.7.cloned.1.call-update
  10.0 0.0 all-gather.9.cloned.1.call-start
  10.1 0.1 multiply_reduce_fusion.7
  10.2 0.1 multiply_reduce_fusion.1
  10.3 0.2 copy-done
  10.5 0.1 multiply_reduce_fusion.5
  10.7 0.0 copy-done.1
  10.7 0.1 multiply_reduce_fusion.3
  10.8 33.6 %reduce-scatter.9.cloned.1.call-done = f32[512,256]{1,0:T(8,128)} async-done(((f32[2048,256]{1,0:T(8,128)}), f32[512,256]{1,0:T(8,128)}) %reduce-scatter.9.cloned.1.call-update) | async-done | bytes 524304 | tf_op jit(solution)/shard_map/reduce_scatter | solution.py:33
  44.5 1.2 multiply_reduce_fusion.2
  45.7 32.5 %reduce-scatter.11.cloned.1.call-done = f32[256,512]{1,0:T(8,128)} async-done(((f32[256,2048]{1,0:T(8,128)}), f32[256,512]{1,0:T(8,128)}) %reduce-scatter.11.cloned.1.call-update) | async-done | bytes 524304 | tf_op jit(solution)/shard_map/reduce_scatter | solution.py:34
  78.2 1.1 multiply_reduce_fusion
  79.3 32.6 %reduce-scatter.5.cloned.1.call-done = f32[512,256]{1,0:T(8,128)} async-done(((f32[2048,256]{1,0:T(8,128)}), f32[512,256]{1,0:T(8,128)}) %reduce-scatter.5.cloned.1.call-update) | async-done | bytes 524304 | tf_op jit(solution)/shard_map/reduce_scatter | solution.py:31
  112.0 1.2 multiply_reduce_fusion.6
  113.2 32.4 %reduce-scatter.7.cloned.1.call-done = f32[512,256]{1,0:T(8,128)} async-done(((f32[2048,256]{1,0:T(8,128)}), f32[512,256]{1,0:T(8,128)}) %reduce-scatter.7.cloned.1.call-update) | async-done | bytes 524304 | tf_op jit(solution)/shard_map/reduce_scatter | solution.py:32
  145.6 1.2 multiply_reduce_fusion.4
  146.7 37.1 %all-reduce = (f32[512,1]{0,1:T(1,128)S(1)}, f32[512,1]{0,1:T(1,128)S(1)}, f32[512,1]{0,1:T(1,128)S(1)}, f32[512,1]{0,1:T(1,128)S(1)}, f32[512,1]{0,1:T(1,128)S(...) all-reduce(f32[512,1]{0,1:T(1,128)S(1)} %bitcast.38, ...), channel_id=1, replica_groups=mesh['replica'=4,'model'=8] {'model'}, use_global_device_ids=true, to_apply=%region_4.0 | all-reduce | flops 4096 | bytes 32768 | tf_op jit(solution)/shard_map/psum | solution.py:60
  183.9 2.3 fusion.10
  186.2 0.0 all-gather.9.cloned.1.call-update
  186.2 0.0 all-gather.11.cloned.1.call-start
  186.3 2.4 fusion.8
  188.7 0.0 all-gather.11.cloned.1.call-update
  188.7 0.0 all-gather.13.cloned.1.call-start
  188.8 1.2 fusion.6
  190.1 0.0 all-gather.13.cloned.1.call-update
  190.1 0.0 all-gather.7.cloned.1.call-start
  190.2 1.3 fusion.12
  191.5 0.0 all-gather.7.cloned.1.call-update
  191.5 10.8 %all-reduce.1 = (f32[2048]{0:T(1024)S(1)}, f32[2048]{0:T(1024)S(1)}) all-reduce(f32[2048]{0:T(1024)S(1)} %bitcast.40, f32[2048]{0:T(1024)S(1)} %bitcast.41), channel_id=1, replica_groups=mesh['replica'=4,'model'=8] {'replica'}, use_global_device_ids=true, to_apply=%region_20.0 | all-reduce | flops 4096 | bytes 32768 | tf_op jit(solution)/shard_map/psum | solution.py:36
  202.3 0.7 fusion.4
  203.0 5.2 %all-gather = bf16[4,1,512]{2,1,0:T(2,128)(2,1)S(1)} all-gather(bf16[1,1,512]{2,1,0:T(2,128)(2,1)S(1)} %reshape.44), channel_id=1, replica_groups=mesh['replica'=4,'model'=8] {'replica'}, dimensions={0}, use_global_device_ids=true | all-gather | bytes 5120 | tf_op jit(solution)/shard_map/all_gather | solution.py:94
  208.2 0.6 copy.36
  208.8 5.3 %all-gather.1 = bf16[4,1,512]{2,1,0:T(2,128)(2,1)S(1)} all-gather(bf16[1,1,512]{2,1,0:T(2,128)(2,1)S(1)} %reshape.46), channel_id=1, replica_groups=mesh['replica'=4,'model'=8] {'replica'}, dimensions={0}, use_global_device_ids=true | all-gather | bytes 5120 | tf_op jit(solution)/shard_map/all_gather | solution.py:95
  214.2 0.6 copy.37
  214.8 3.6 %all-gather.11.cloned.1.call-done = bf16[2048,256]{1,0:T(8,128)(2,1)} async-done(((bf16[512,256]{1,0:T(8,128)(2,1)}), bf16[2048,256]{1,0:T(8,128)(2,1)}) %all-gather.11.cloned.1.call-update) | async-done | bytes 1048592 | tf_op jit(solution)/shard_map/all_gather | solution.py:92
  218.3 18.8 %all-gather.13.cloned.1.call-done = bf16[256,2048]{1,0:T(8,128)(2,1)} async-done(((bf16[256,512]{1,0:T(8,128)(2,1)}), bf16[256,2048]{1,0:T(8,128)(2,1)}) %all-gather.13.cloned.1.call-update) | async-done | bytes 1048592 | tf_op jit(solution)/shard_map/all_gather | solution.py:93
  237.2 18.9 %all-gather.7.cloned.1.call-done = bf16[2048,256]{1,0:T(8,128)(2,1)} async-done(((bf16[512,256]{1,0:T(8,128)(2,1)}), bf16[2048,256]{1,0:T(8,128)(2,1)}) %all-gather.7.cloned.1.call-update) | async-done | bytes 1048592 | tf_op jit(solution)/shard_map/all_gather | solution.py:90
  256.0 2.4 copy.42
  258.4 1.0 copy.43
  259.4 1.0 copy.44
  260.3 1.0 copy.45
  (44 shorter events, 0.2 us)
Async XLA Ops:
  7.2 37.3 %reduce-scatter.9.cloned.1.call-start = ((), (), s32[]{:S(2)}) async-start(), calls=%async_computation.8 | async-start | bytes 2621440 | tf_op jit(solution)/shard_map/reduce_scatter | solution.py:33
  7.9 70.3 %reduce-scatter.11.cloned.1.call-start = ((), (), s32[]{:S(2)}) async-start(), calls=%async_computation.10 | async-start | bytes 2621440 | tf_op jit(solution)/shard_map/reduce_scatter | solution.py:34
  8.7 103.3 %reduce-scatter.5.cloned.1.call-start = ((), (), s32[]{:S(2)}) async-start(), calls=%async_computation.4 | async-start | bytes 2621440 | tf_op jit(solution)/shard_map/reduce_scatter | solution.py:31
  8.7 1.3 copy-start.3
  8.7 1.5 copy-start.2
  9.4 1.1 copy-start
  9.4 1.3 copy-start.1
  9.4 136.1 %reduce-scatter.7.cloned.1.call-start = ((), (), s32[]{:S(2)}) async-start(), calls=%async_computation.6 | async-start | bytes 2621440 | tf_op jit(solution)/shard_map/reduce_scatter | solution.py:32
  10.0 173.8 %copy-start.10 = (f32[512,256]{1,0:T(8,128)S(1)}, f32[512,256]{1,0:T(8,128)}, u32[]{:S(2)}) copy-start(f32[512,256]{1,0:T(8,128)} %param.31) | copy-start | bytes 1572868
  10.0 204.8 %all-gather.9.cloned.1.call-start = ((), (), s32[]{:S(2)}) async-start(), calls=%async_computation.7 | async-start | bytes 1310720 | tf_op jit(solution)/shard_map/all_gather | solution.py:91
  79.3 106.9 %copy-start.6 = (f32[512,256]{1,0:T(8,128)S(1)}, f32[512,256]{1,0:T(8,128)}, u32[]{:S(2)}) copy-start(f32[512,256]{1,0:T(8,128)} %reduce-scatter.9.cloned.1.call-done) | copy-start | bytes 1572868
  186.2 2.6 copy-start.5
  186.2 2.6 copy-start.11
  186.2 32.1 %all-gather.11.cloned.1.call-start = ((), (), s32[]{:S(2)}) async-start(), calls=%async_computation.9 | async-start | bytes 1310720 | tf_op jit(solution)/shard_map/all_gather | solution.py:92
  188.7 1.5 copy-start.4
  188.7 1.5 copy-start.12
  188.7 48.5 %all-gather.13.cloned.1.call-start = ((), (), s32[]{:S(2)}) async-start(), calls=%async_computation.11 | async-start | bytes 1310720 | tf_op jit(solution)/shard_map/all_gather | solution.py:93
  190.0 1.5 copy-start.13
  190.0 1.5 copy-start.14
  190.0 12.3 %copy-start.15 = (f32[512]{0:T(512)S(1)}, f32[512]{0:T(512)}, u32[]{:S(2)}) copy-start(f32[512]{0:T(512)} %param.29) | copy-start | bytes 6148
  190.0 12.3 %copy-start.16 = (f32[512]{0:T(512)S(1)}, f32[512]{0:T(512)}, u32[]{:S(2)}) copy-start(f32[512]{0:T(512)} %param.35) | copy-start | bytes 6148
  190.0 12.3 %copy-start.17 = (f32[512]{0:T(512)S(1)}, f32[512]{0:T(512)}, u32[]{:S(2)}) copy-start(f32[512]{0:T(512)} %param.28) | copy-start | bytes 6148
  190.1 12.3 %copy-start.18 = (f32[512]{0:T(512)S(1)}, f32[512]{0:T(512)}, u32[]{:S(2)}) copy-start(f32[512]{0:T(512)} %param.34) | copy-start | bytes 6148
  190.1 65.9 %all-gather.7.cloned.1.call-start = ((), (), s32[]{:S(2)}) async-start(), calls=%async_computation.5 | async-start | bytes 1310720 | tf_op jit(solution)/shard_map/all_gather | solution.py:90
  214.8 43.6 %copy-start.7 = (bf16[2048,256]{1,0:T(8,128)(2,1)S(1)}, bf16[2048,256]{1,0:T(8,128)(2,1)}, u32[]{:S(2)}) copy-start(bf16[2048,256]{1,0:T(8,128)(2,1)} %all-gather.9.cloned.1.call-done) | copy-start | bytes 3145732
  256.0 3.3 %copy-start.8 = (bf16[2048,256]{1,0:T(8,128)(2,1)S(1)}, bf16[2048,256]{1,0:T(8,128)(2,1)}, u32[]{:S(2)}) copy-start(bf16[2048,256]{1,0:T(8,128)(2,1)} %all-gather.11.cloned.1.call-done) | copy-start | bytes 3145732
  258.4 1.9 copy-start.9
Sparse Core Ops, SparseCore 0:
  10.5 33.9 reduce-scatter.8
  47.0 31.1 reduce-scatter.10
  80.7 31.1 reduce-scatter.4
  114.3 31.1 reduce-scatter.6
  186.3 13.1 all-gather.8
  201.5 16.7 all-gather.10
  220.5 16.6 all-gather.12
  239.3 16.6 all-gather.6
where the time goes:
time: 269 us; the launch traced here: 268 us
  waiting for transfers between devices  175 us (65%)
  blocking collectives  58.4 us (22%)
  between operations  14.4 us (5%)
  other arithmetic  13.2 us (5%)
  local copies, waits for them, and re-layouts  6.78 us (3%)
    psum x1, blocking collectives, shards(): lax.psum((jnp.sum(master_query * master_query, axis=1, keepdims=True), jn...  37.1 us
    reduce_scatter x1, waiting for transfers between devices, shards(): lax.psum_scatter(partial_value[0], 'replica', scatter_dimension=0, tiled=...  33.6 us
    reduce_scatter x1, waiting for transfers between devices, shards(): lax.psum_scatter(partial_query[0], 'replica', scatter_dimension=0, tiled=...  32.6 us
    reduce_scatter x1, waiting for transfers between devices, shards(): lax.psum_scatter(partial_mixed[0], 'replica', scatter_dimension=1, tiled=...  32.5 us
    reduce_scatter x1, waiting for transfers between devices, shards(): lax.psum_scatter(partial_key[0], 'replica', scatter_dimension=0, tiled=True)  32.4 us
    all_gather x1, waiting for transfers between devices, shards(): lax.all_gather(stepped_query.astype(jnp.bfloat16), 'replica', axis=0, til...  18.9 us
    all_gather x1, waiting for transfers between devices, shards(): lax.all_gather(stepped_mixed.astype(jnp.bfloat16), 'replica', axis=1, til...  18.8 us
    psum x1, blocking collectives, shards(): lax.psum((partial_norm[0], partial_bias[0]), 'replica')  10.8 us
  transfers between devices with their start and end apart: 8, of which 7 were waited for; matrix products, arithmetic and copies ran while one was open for 4% of the time, Pallas kernels for 0%

commit v1 on v0

v1 whole, which is shorter than its diff:
```python
import jax
import jax.numpy as jnp
from jax import lax
from jax.sharding import PartitionSpec as P


learn_rate = 0.015
hold_rate = 0.8

half_bound = 8.0
wire_scale = 60000.0 / half_bound**1.5


names = ("query", "key", "value", "mixed")


def block_of(whole, index, count, axis):
    if axis == 0:
        split = whole.reshape(count, whole.shape[0] // count, whole.shape[1])
        return lax.dynamic_index_in_dim(split, index, axis=0, keepdims=False)
    size = whole.shape[1] // count
    return lax.dynamic_slice_in_dim(whole, index * size, size, axis=1)


def put_block(whole, block, index, count, axis):
    if axis == 0:
        split = whole.reshape(count, whole.shape[0] // count, whole.shape[1])
        return lax.dynamic_update_index_in_dim(split, block[None], index, axis=0).reshape(whole.shape)
    return lax.dynamic_update_slice_in_dim(whole, block, index * block.shape[1], axis=1)


def shards(*args):
    partial = dict(zip(names, (a[0] for a in args[0:4])))
    partial_vectors = jnp.stack([args[4][0], args[5][0]])
    master = dict(zip(names, args[6:10]))
    master_vectors = jnp.stack(args[10:12])
    memory = dict(zip(names, args[12:16]))
    memory_vectors = jnp.stack(args[16:18])
    axis_of = {"query": 0, "key": 0, "value": 0, "mixed": 1}

    count = lax.axis_size("replica")
    width = 2 if count % 2 == 0 else 1
    chips = count // width
    place = lax.axis_index("replica")
    chip, core = place // width, place % width
    models = lax.axis_size("model")
    mean_rate = count ** (-0.5)

    def to_pair(value):
        return lax.ppermute(value, "replica", [(i, i ^ 1) for i in range(count)])

    def to_chip(value, step):
        pairs = [
            (i, (i // width + step) % chips * width + i % width) for i in range(count)
        ]
        return lax.ppermute(value, "replica", pairs)

    def after(value, *others):
        return lax.optimization_barrier((value, *others))[0]

    def encode(value):
        size = jnp.abs(value)
        root = size * lax.rsqrt(jnp.maximum(size, 1e-30))
        return (value * root * wire_scale).astype(jnp.float16)

    def decode(code):
        code = code.astype(jnp.float32)
        size = jnp.exp(jnp.log(jnp.abs(code) * (1.0 / wire_scale)) * (2.0 / 3.0))
        return jnp.where(code < 0, -size, size)

    def other(step):
        return (chip + step) % chips * width + core

    def paired(n, step):
        own = block_of(partial[n], other(step), count, axis_of[n])
        if width == 1:
            return own
        theirs = block_of(partial[n], other(step) ^ 1, count, axis_of[n])
        return own + to_pair(theirs)

    own_vectors = jnp.concatenate([master_vectors, memory_vectors])
    vector_sum, vector_all = partial_vectors, jnp.zeros((count,) + own_vectors.shape, jnp.float32)
    vector_all = lax.dynamic_update_index_in_dim(vector_all, own_vectors[None], place, axis=0)
    packed = jnp.concatenate([partial_vectors.reshape(-1), own_vectors.reshape(-1)])
    split = partial_vectors.size
    vector_got = [to_chip(packed, step) for step in range(1, chips)]

    arrived = {}
    for n in names:
        arrived[n] = []
        for step in range(1, chips):
            arrived[n].append(to_chip(encode(paired(n, step)), step))

    for step, got in enumerate(vector_got, 1):
        got = after(got, *arrived["query"])
        vector_sum = vector_sum + got[:split].reshape(partial_vectors.shape)
        vector_all = lax.dynamic_update_index_in_dim(
            vector_all,
            got[split:].reshape(own_vectors.shape)[None],
            (chip - step) % chips * width + core,
            axis=0,
        )

    mean, outs = {}, {}

    def reduce(n, *others):
        total = paired(n, 0)
        for piece in arrived[n]:
            total = total + decode(after(piece, *others))
        mean[n] = total * mean_rate
        return jnp.sum(mean[n] * mean[n], axis=1 - axis_of[n])

    def own_size(n):
        held = after(master[n], *arrived["query"])
        return jnp.sum(held * held, axis=1 - axis_of[n])

    def finish(n, own, slope):
        ratio = jnp.sqrt(own) * lax.rsqrt(slope + 1e-06)
        scaled = mean[n] * jnp.expand_dims(ratio, 1 - axis_of[n])
        state_new = hold_rate * memory[n] + (1.0 - hold_rate) * scaled * scaled
        stepped = master[n] - learn_rate * scaled * lax.rsqrt(state_new + 1e-06)
        compute = stepped.astype(jnp.bfloat16)
        pieces = [(compute, place)]
        for step in range(1, chips):
            pieces.append((to_chip(compute, step), (chip - step) % chips * width + core))
        outs[n] = (pieces, stepped, state_new)
        return compute

    def gather(n, *others):
        pieces, stepped, state_new = outs[n]
        whole = jnp.zeros(partial[n].shape, jnp.bfloat16)
        for piece, index in pieces:
            whole = put_block(whole, piece, index, count, axis_of[n])
            if width == 2:
                whole = put_block(whole, to_pair(piece), index ^ 1, count, axis_of[n])
        outs[n] = (whole, stepped, state_new)

    def stages(value):
        if models & (models - 1):
            return [lax.psum(value, "model")]
        found, bit = [], 1
        while bit < models:
            got = lax.ppermute(value, "model", [(i, i ^ bit) for i in range(models)])
            value = value + got
            found.append(value)
            bit *= 2
        return found

    slope_q = reduce("query")
    slope_k = reduce("key")
    first = stages(jnp.stack([own_size("query"), own_size("key"), slope_q, slope_k]))
    slope_v = reduce("value", first[0])
    slope_m = reduce("mixed", first[-1])
    second = stages(jnp.stack([own_size("value"), own_size("mixed"), slope_v, slope_m]))
    total = first[-1]
    finish("query", total[0], total[2])
    finish("key", total[1], total[3])
    total = second[-1]
    finish("value", total[0], total[2])
    finish("mixed", total[1], total[3])
    for n in names:
        gather(n)

    if width == 2:
        vector_sum = vector_sum + to_pair(vector_sum)
        theirs = to_pair(vector_all)
        held = (jnp.arange(count) % width == core)[:, None, None]
        vector_all = jnp.where(held, vector_all, theirs)
    vector_mean = vector_sum * mean_rate
    vector_all = vector_all.transpose(1, 0, 2).reshape(4, -1)
    state_whole = hold_rate * vector_all[2:] + (1.0 - hold_rate) * vector_mean * vector_mean
    stepped_whole = vector_all[:2] - learn_rate * vector_mean * lax.rsqrt(state_whole + 1e-06)
    compute_vectors = stepped_whole.astype(jnp.bfloat16)
    own = args[10].shape[0]
    stepped_own = lax.dynamic_slice_in_dim(stepped_whole, place * own, own, axis=1)
    state_own = lax.dynamic_slice_in_dim(state_whole, place * own, own, axis=1)
    return (
        *(outs[n][0] for n in names),
        compute_vectors[0],
        compute_vectors[1],
        *(outs[n][1] for n in names),
        stepped_own[0],
        stepped_own[1],
        *(outs[n][2] for n in names),
        state_own[0],
        state_own[1],
    )


def solution(mesh):
    rows, columns = P("replica", "model"), P("model", "replica")
    in_specs = (
        *(P("replica", None, "model"),) * 3,
        P("replica", "model", None),
        *(P("replica", None),) * 2,
        *((rows,) * 3 + (columns,) + (P("replica"),) * 2) * 2,
    )
    out_specs = (
        *(P(None, "model"),) * 3,
        P("model", None),
        P(),
        P(),
        *((rows,) * 3 + (columns,) + (P("replica"),) * 2) * 2,
    )

    return jax.shard_map(shards, mesh=mesh, in_specs=in_specs, out_specs=out_specs, check_vma=False)
```

time: 269 us -> 89.1 us (0.33)
  waiting for transfers between devices: 175 us -> 31.2 us
  blocking collectives: 58.4 us -> 0 us
  starting transfers between devices: 0.31 us -> 26.5 us
  between operations: 14.4 us -> 1.32 us
  other arithmetic: 13.2 us -> 19.1 us
  local copies, waits for them, and re-layouts: 6.78 us -> 10.7 us
    reduce_scatter x4 -> x0, waiting for transfers between devices: 131 us -> none  [the longest x1 33.6 us: shards(): lax.psum_scatter(partial_value[0], 'replica', scatter_dimension=0, tiled=...]
    psum x2 -> x0, blocking collectives: 47.8 us -> none  [the longest x1 37.1 us: shards(): lax.psum((jnp.sum(master_query * master_query, axis=1, keepdims=True), jn...]
    all_gather x4 -> x0, waiting for transfers between devices: 41.2 us -> none  [the longest x1 18.9 us: shards(): lax.all_gather(stepped_query.astype(jnp.bfloat16), 'replica', axis=0, til...]
    ppermute x0 -> x33, waiting for transfers between devices: none -> 31.2 us  [the longest x9 22.8 us: to_chip(): return lax.ppermute(value, 'replica', pairs)]
    ppermute x0 -> x33, starting transfers between devices: none -> 26.5 us  [the longest x6 11.7 us: stages(): got = lax.ppermute(value, 'model', [(i, i ^ bit) for i in range(models)])]
    all_gather x2 -> x0, blocking collectives: 10.5 us -> none  [the longest x1 5.33 us: shards(): lax.all_gather(stepped_bias.astype(jnp.bfloat16), 'replica', axis=0, tile...]
    unnamed x46, local copies, waits for them, and re-layouts: 6.78 us -> 1.86 us
    dynamic_update_slice x0 -> x4, other arithmetic: none -> 4.85 us  [the longest x3 3.65 us: put_block(): lax.dynamic_update_index_in_dim(split, block[None], index, axis=0)]
  transfers between devices with their start and end apart: 8 -> 33, of which waited for: 7 -> 11; matrix products, arithmetic and copies ran while one was open for 4% -> 30% of each run, Pallas kernels for 0% -> 0%
where the time goes in v1:
time: 89.1 us; the launch traced here: 88.7 us
  waiting for transfers between devices  31.2 us (35%)
  starting transfers between devices  26.5 us (30%)
  other arithmetic  19.1 us (21%)
  local copies, waits for them, and re-layouts  10.7 us (12%)
  between operations  1.32 us (1%)
    ppermute x9, waiting for transfers between devices, to_chip(): return lax.ppermute(value, 'replica', pairs)  22.8 us
    ppermute x6, starting transfers between devices, stages(): got = lax.ppermute(value, 'model', [(i, i ^ bit) for i in range(models)])  11.7 us
    ppermute x9, starting transfers between devices, to_chip(): return lax.ppermute(value, 'replica', pairs)  11.4 us
    ppermute x6, waiting for transfers between devices, stages(): got = lax.ppermute(value, 'model', [(i, i ^ bit) for i in range(models)])  7.1 us
    convert_element_type x4, other arithmetic, encode(): return (value * root * wire_scale).astype(jnp.float16)  6.37 us
    reduce_sum x3, other arithmetic, reduce(): return jnp.sum(mean[n] * mean[n], axis=1 - axis_of[n])  5.38 us
    squeeze x3, local copies, waits for them, and re-layouts, block_of(): return lax.dynamic_index_in_dim(split, index, axis=0, keepdims=False)  4.33 us
    dynamic_update_slice x3, other arithmetic, put_block(): lax.dynamic_update_index_in_dim(split, block[None], index, axis=0)  3.65 us
  transfers between devices with their start and end apart: 33, of which 11 were waited for; matrix products, arithmetic and copies ran while one was open for 30% of the time, Pallas kernels for 0%

profile of v1, /device:TPU:0, one launch (start us, length us, event | category | flops | bytes accessed | tf_op | source)
XLA Modules:
  0.0 88.7 jit_solution(18337368639624035201)
XLA Ops:
  0.7 0.9 fusion.26
  1.6 0.8 fusion.40
  2.3 3.1 %collective-permute-start.30 = (f32[6144]{0:T(1024)S(1)}, f32[6144]{0:T(1024)S(1)}, u32[]{:S(2)}, u32[]{:S(2)}) collective-permute-start(f32[6144]{0:T(1024)S(1)} %pad_maximum_fusion), channel_id=1, source_target_pairs={{0,16},{8,24},{16,0},{24,8},{1,17},{9,25},{17,1},{25,9},{2,18},{10... | collective-permute-start | bytes 73736 | tf_op jit(solution)/shard_map/ppermute | solution.py:56
  5.4 2.2 %dynamic-slice_bitcast_fusion.7 = (f32[512,256]{1,0:T(8,128)}, f32[512,256]{1,0:T(8,128)}) fusion(f32[4,512,256]{2,1,0:T(8,128)} %bitcast.120, s32[]{:T(128)S(6)} %select_n.162, s32[]{:T(128)S(6)} %select_n.165), kind=kLoop, calls=%fused_computation.71 | loop fusion | bytes 2097160 | tf_op jit(solution)/shard_map/jit(dynamic_index_in_dim)/squeeze | solution.py:20
  7.6 1.0 %dynamic-slice_bitcast_fusion.5 = (f32[512,256]{1,0:T(8,128)}, f32[512,256]{1,0:T(8,128)}) fusion(f32[4,512,256]{2,1,0:T(8,128)S(1)} %bitcast.117, s32[]{:T(128)S(6)} %select_n.162, s32[]{:T(128)S(6)} %select_n.165), kind=kLoop, calls=%fused_computation.65 | loop fusion | bytes 2097160 | tf_op jit(solution)/shard_map/jit(dynamic_index_in_dim)/squeeze | solution.py:20
  8.7 0.5 collective-permute-start.4
  9.2 2.4 %dynamic-slice_bitcast_fusion.1 = (f32[256,512]{1,0:T(8,128)}, f32[256,512]{1,0:T(8,128)}) fusion(f32[1,256,2048]{2,1,0:T(8,128)} %param.21, s32[]{:T(128)S(6)} %select_n.175, s32[]{:T(128)S(6)} %select_n.177), kind=kLoop, calls=%fused_computation.53 | loop fusion | bytes 2097160 | tf_op jit(solution)/shard_map/dynamic_slice | solution.py:22
  11.6 1.0 %dynamic-slice_bitcast_fusion.3 = (f32[512,256]{1,0:T(8,128)}, f32[512,256]{1,0:T(8,128)}) fusion(f32[4,512,256]{2,1,0:T(8,128)S(1)} %bitcast.125, s32[]{:T(128)S(6)} %select_n.162, s32[]{:T(128)S(6)} %select_n.165), kind=kLoop, calls=%fused_computation.59 | loop fusion | bytes 2097160 | tf_op jit(solution)/shard_map/jit(dynamic_index_in_dim)/squeeze | solution.py:20
  12.6 0.5 collective-permute-start.16
  13.5 1.2 %multiply_convert_fusion.3 = f16[512,256]{1,0:T(8,128)(2,1)S(1)} fusion(f32[512,256]{1,0:T(8,128)S(1)} %collective-permute-done.1, f32[4,512,256]{2,1,0:T(8,128)} %bitcast.121, s32[]{:T(128)S(6)} %select_n.164), kind=kLoop, calls=%fused_computation.69 | loop fusion | flops 917504 | bytes 1310724 | tf_op jit(solution)/shard_map/convert_element_type | solution.py:64
  14.7 0.8 copy-done.14
  15.9 1.9 %multiply_convert_fusion.2 = f16[512,256]{1,0:T(8,128)(2,1)} fusion(f32[512,256]{1,0:T(8,128)} %copy-done.14, f32[4,512,256]{2,1,0:T(8,128)S(1)} %bitcast.118, s32[]{:T(128)S(6)} %select_n.164), kind=kLoop, calls=%fused_computation.63 | loop fusion | flops 917504 | bytes 1310724 | tf_op jit(solution)/shard_map/convert_element_type | solution.py:64
  18.0 2.1 %multiply_convert_fusion.1 = f16[512,256]{1,0:T(8,128)(2,1)} fusion(f32[512,256]{1,0:T(8,128)} %collective-permute-done.16, f32[4,512,256]{2,1,0:T(8,128)} %bitcast.123, s32[]{:T(128)S(6)} %select_n.164), kind=kLoop, calls=%fused_computation.57 | loop fusion | flops 917504 | bytes 1310724 | tf_op jit(solution)/shard_map/convert_element_type | solution.py:64
  20.0 1.9 %collective-permute-start.5 = (f16[512,256]{1,0:T(8,128)(2,1)}, f16[512,256]{1,0:T(8,128)(2,1)}, u32[]{:S(2)}, u32[]{:S(2)}) collective-permute-start(f16[512,256]{1,0:T(8,128)(2,1)} %multiply_convert_fusion.2), channel_id=1, source_target_pairs={{0,16},{8,24},{16,0},{24,8},{1,17},{9,25},{17,1},{25,9},{2,18},{10... | collective-permute-start | bytes 786440 | tf_op jit(solution)/shard_map/ppermute | solution.py:56
  22.0 1.2 %multiply_convert_fusion = f16[256,512]{1,0:T(8,128)(2,1)S(1)} fusion(f32[256,512]{1,0:T(8,128)S(1)} %collective-permute-done.19, f32[1,256,2048]{2,1,0:T(8,128)} %param.21, s32[]{:T(128)S(6)} %select_n.176), kind=kLoop, calls=%fused_computation.51 | loop fusion | flops 917504 | bytes 1310724 | tf_op jit(solution)/shard_map/convert_element_type | solution.py:64
  23.3 3.9 %collective-permute-done.2 = f16[512,256]{1,0:T(8,128)(2,1)} collective-permute-done((f16[512,256]{1,0:T(8,128)(2,1)S(1)}, f16[512,256]{1,0:T(8,128)(2,1)}, u32[]{:S(2)}, u32[]{:S(2)}) %collective-permute-start.2) | collective-permute-done | bytes 262176 | tf_op jit(solution)/shard_map/ppermute | solution.py:56
  27.4 4.6 %collective-permute-done.5 = f16[512,256]{1,0:T(8,128)(2,1)} collective-permute-done((f16[512,256]{1,0:T(8,128)(2,1)}, f16[512,256]{1,0:T(8,128)(2,1)}, u32[]{:S(2)}, u32[]{:S(2)}) %collective-permute-start.5) | collective-permute-done | bytes 262176 | tf_op jit(solution)/shard_map/ppermute | solution.py:56
  32.5 1.8 %collective-permute-start.17 = (f16[512,256]{1,0:T(8,128)(2,1)}, f16[512,256]{1,0:T(8,128)(2,1)}, u32[]{:S(2)}, u32[]{:S(2)}) collective-permute-start(f16[512,256]{1,0:T(8,128)(2,1)} %multiply_convert_fusion.1), channel_id=1, source_target_pairs={{0,16},{8,24},{16,0},{24,8},{1,17},{9,25},{17,1},{25,9},{2,18},{10... | collective-permute-start | bytes 786440 | tf_op jit(solution)/shard_map/ppermute | solution.py:56
  34.3 2.1 %multiply_reduce_fusion.4 = (f32[512]{0:T(512)S(1)}, f32[512,256]{1,0:T(8,128)S(1)}, f32[512]{0:T(512)S(1)}, f32[512,256]{1,0:T(8,128)S(1)}) fusion(f16[512,256]{1,0:T(8,128)(2,1)} %collective-permute-done.5, f32[512,256]{1,0:T(8,128)} %collective-permute-done.3, f32[4,512,256]{2,1,0:T(8,128)S(1)} %bitcast.119, s32[]{:T(128)S(6)} %select_n.161, ...), kind=kLoop, calls=%fused_computation.62 | loop fusion | flops 3144704 | bytes 3674116 | tf_op jit(solution)/shard_map/reduce_sum | solution.py:111
  36.5 1.6 %collective-permute-start.6 = (f32[4,512]{1,0:T(4,128)S(1)}, f32[4,512]{1,0:T(4,128)S(1)}, u32[]{:S(2)}, u32[]{:S(2)}) collective-permute-start(f32[4,512]{1,0:T(4,128)S(1)} %pad_maximum_fusion.2), channel_id=1, source_target_pairs={{0,1},{1,0},{2,3},{3,2},{4,5},{5,4},{6,7},{7,6},{8,9},{9,8},{10,11... | collective-permute-start | bytes 24584 | tf_op jit(solution)/shard_map/ppermute | solution.py:143
  38.2 2.0 %collective-permute-done.6 = f32[4,512]{1,0:T(4,128)S(1)} collective-permute-done((f32[4,512]{1,0:T(4,128)S(1)}, f32[4,512]{1,0:T(4,128)S(1)}, u32[]{:S(2)}, u32[]{:S(2)}) %collective-permute-start.6) | collective-permute-done | bytes 8224 | tf_op jit(solution)/shard_map/ppermute | solution.py:143
  40.2 1.6 %collective-permute-start.7 = (f32[4,512]{1,0:T(4,128)S(1)}, f32[4,512]{1,0:T(4,128)S(1)}, u32[]{:S(2)}, u32[]{:S(2)}) collective-permute-start(f32[4,512]{1,0:T(4,128)S(1)} %fusion.42), channel_id=1, source_target_pairs={{0,2},{1,3},{2,0},{3,1},{4,6},{5,7},{6,4},{7,5},{8,10},{9,11},{10,... | collective-permute-start | bytes 24584 | tf_op jit(solution)/shard_map/ppermute | solution.py:143
  42.0 3.2 %collective-permute-done.17 = f16[512,256]{1,0:T(8,128)(2,1)} collective-permute-done((f16[512,256]{1,0:T(8,128)(2,1)}, f16[512,256]{1,0:T(8,128)(2,1)}, u32[]{:S(2)}, u32[]{:S(2)}) %collective-permute-start.17) | collective-permute-done | bytes 262176 | tf_op jit(solution)/shard_map/ppermute | solution.py:56
  45.2 0.5 collective-permute-start.31
  45.7 2.7 %collective-permute-start.8 = (f32[4,512]{1,0:T(4,128)S(1)}, f32[4,512]{1,0:T(4,128)S(1)}, u32[]{:S(2)}, u32[]{:S(2)}) collective-permute-start(f32[4,512]{1,0:T(4,128)S(1)} %fusion.55), channel_id=1, source_target_pairs={{0,4},{1,5},{2,6},{3,7},{4,0},{5,1},{6,2},{7,3},{8,12},{9,13},{10,... | collective-permute-start | bytes 24584 | tf_op jit(solution)/shard_map/ppermute | solution.py:143
  48.3 1.6 %multiply_reduce_fusion.1 = (f32[512]{0:T(512)S(1)}, f32[512,256]{1,0:T(8,128)S(1)}) fusion(f16[512,256]{1,0:T(8,128)(2,1)} %collective-permute-done.17, f32[512,256]{1,0:T(8,128)} %collective-permute-done.15, f32[4,512,256]{2,1,0:T(8,128)} %bitcast.124, s32[]{:T(128)S(6)} %select_n.161), kind=kLoop, calls=%fused_computation.54 | loop fusion | flops 1572352 | bytes 1837060 | tf_op jit(solution)/shard_map/reduce_sum | solution.py:111
  50.5 1.2 %bitcast_dynamic-update-slice_fusion.11 = (bf16[4,512,256]{2,1,0:T(8,128)(2,1)S(1)}, bf16[512,256]{1,0:T(8,128)(2,1)S(1)}, f32[512,256]{1,0:T(8,128)}, f32[512,256]{1,0:T(8,128)}) fusion(bf16[4,512,256]{2,1,0:T(8,128)(2,1)S(1)} %broadcast.101.clone, s32[]{:T(128)S(6)} %select_n.168, f32[512,256]{1,0:T(8,128)S(1)} %copy-done.3, ...), kind=kLoop, calls=%fused_computation.83 | loop fusion | flops 1310720 | bytes 3147780 | tf_op jit(solution)/shard_map/jit(dynamic_update_index_in_dim)/dynamic_update_slice | solution.py:28
  51.7 0.5 collective-permute-start.10
  52.3 1.2 %bitcast_dynamic-update-slice_fusion.7 = (bf16[4,512,256]{2,1,0:T(8,128)(2,1)S(1)}, bf16[512,256]{1,0:T(8,128)(2,1)S(1)}, f32[512,256]{1,0:T(8,128)}, f32[512,256]{1,0:T(8,128)}) fusion(bf16[4,512,256]{2,1,0:T(8,128)(2,1)S(1)} %broadcast.101.clone.1, s32[]{:T(128)S(6)} %select_n.168, f32[512,256]{1,0:T(8,128)S(1)} %copy-done.5, ...), kind=kLoop, calls=%fused_computation.79 | loop fusion | flops 1310720 | bytes 3147780 | tf_op jit(solution)/shard_map/jit(dynamic_update_index_in_dim)/dynamic_update_slice | solution.py:28
  53.8 1.6 %multiply_reduce_fusion = (f32[512]{0:T(512)S(1)}, f32[256,512]{1,0:T(8,128)S(1)}) fusion(f16[256,512]{1,0:T(8,128)(2,1)} %collective-permute-done.20, f32[256,512]{1,0:T(8,128)} %collective-permute-done.18, f32[1,256,2048]{2,1,0:T(8,128)} %param.21, s32[]{:T(128)S(6)} %select_n.174), kind=kLoop, calls=%fused_computation.50 | loop fusion | flops 1572352 | bytes 1837060 | tf_op jit(solution)/shard_map/reduce_sum | solution.py:111
  55.4 1.6 %collective-permute-start.21 = (f32[4,512]{1,0:T(4,128)S(1)}, f32[4,512]{1,0:T(4,128)S(1)}, u32[]{:S(2)}, u32[]{:S(2)}) collective-permute-start(f32[4,512]{1,0:T(4,128)S(1)} %pad_maximum_fusion.3), channel_id=1, source_target_pairs={{0,1},{1,0},{2,3},{3,2},{4,5},{5,4},{6,7},{7,6},{8,9},{9,8},{10,11... | collective-permute-start | bytes 24584 | tf_op jit(solution)/shard_map/ppermute | solution.py:143
  57.1 2.1 %collective-permute-done.21 = f32[4,512]{1,0:T(4,128)S(1)} collective-permute-done((f32[4,512]{1,0:T(4,128)S(1)}, f32[4,512]{1,0:T(4,128)S(1)}, u32[]{:S(2)}, u32[]{:S(2)}) %collective-permute-start.21) | collective-permute-done | bytes 8224 | tf_op jit(solution)/shard_map/ppermute | solution.py:143
  59.1 1.5 %collective-permute-start.13 = (bf16[512,256]{1,0:T(8,128)(2,1)S(1)}, bf16[512,256]{1,0:T(8,128)(2,1)S(1)}, u32[]{:S(2)}, u32[]{:S(2)}) collective-permute-start(bf16[512,256]{1,0:T(8,128)(2,1)S(1)} %get-tuple-element.49), channel_id=1, source_target_pairs={{0,16},{8,24},{16,0},{24,8},{1,17},{9,25},{17,1},{25,9},{2,18},{10... | collective-permute-start | bytes 786440 | tf_op jit(solution)/shard_map/ppermute | solution.py:56
  60.7 1.6 %collective-permute-start.22 = (f32[4,512]{1,0:T(4,128)S(1)}, f32[4,512]{1,0:T(4,128)S(1)}, u32[]{:S(2)}, u32[]{:S(2)}) collective-permute-start(f32[4,512]{1,0:T(4,128)S(1)} %fusion.41), channel_id=1, source_target_pairs={{0,2},{1,3},{2,0},{3,1},{4,6},{5,7},{6,4},{7,5},{8,10},{9,11},{10,... | collective-permute-start | bytes 24584 | tf_op jit(solution)/shard_map/ppermute | solution.py:143
  62.4 0.6 slice_reduce_fusion
  63.1 1.4 %collective-permute-done.22 = f32[4,512]{1,0:T(4,128)S(1)} collective-permute-done((f32[4,512]{1,0:T(4,128)S(1)}, f32[4,512]{1,0:T(4,128)S(1)}, u32[]{:S(2)}, u32[]{:S(2)}) %collective-permute-start.22) | collective-permute-done | bytes 8224 | tf_op jit(solution)/shard_map/ppermute | solution.py:143
  64.5 2.6 %collective-permute-start.23 = (f32[4,512]{1,0:T(4,128)S(1)}, f32[4,512]{1,0:T(4,128)S(1)}, u32[]{:S(2)}, u32[]{:S(2)}) collective-permute-start(f32[4,512]{1,0:T(4,128)S(1)} %fusion.54), channel_id=1, source_target_pairs={{0,4},{1,5},{2,6},{3,7},{4,0},{5,1},{6,2},{7,3},{8,12},{9,13},{10,... | collective-permute-start | bytes 24584 | tf_op jit(solution)/shard_map/ppermute | solution.py:143
  67.1 0.7 fusion.52
  67.8 1.3 %collective-permute-done.23 = f32[4,512]{1,0:T(4,128)S(1)} collective-permute-done((f32[4,512]{1,0:T(4,128)S(1)}, f32[4,512]{1,0:T(4,128)S(1)}, u32[]{:S(2)}, u32[]{:S(2)}) %collective-permute-start.23) | collective-permute-done | bytes 8224 | tf_op jit(solution)/shard_map/ppermute | solution.py:143
  69.2 1.2 %bitcast_dynamic-update-slice_fusion.3 = (bf16[4,512,256]{2,1,0:T(8,128)(2,1)S(1)}, bf16[512,256]{1,0:T(8,128)(2,1)S(1)}, f32[512,256]{1,0:T(8,128)}, f32[512,256]{1,0:T(8,128)}) fusion(bf16[4,512,256]{2,1,0:T(8,128)(2,1)S(1)} %broadcast.101.clone.2, s32[]{:T(128)S(6)} %select_n.168, f32[512,256]{1,0:T(8,128)S(1)} %copy-done.7, ...), kind=kLoop, calls=%fused_computation.75 | loop fusion | flops 1310720 | bytes 3147780 | tf_op jit(solution)/shard_map/jit(dynamic_update_index_in_dim)/dynamic_update_slice | solution.py:28
  70.6 1.2 %constant_dynamic-update-slice_fusion.3 = (bf16[256,2048]{1,0:T(8,128)(2,1)S(1)}, bf16[256,512]{1,0:T(8,128)(2,1)S(1)}, f32[256,512]{1,0:T(8,128)}, f32[256,512]{1,0:T(8,128)}) fusion(bf16[256,2048]{1,0:T(8,128)(2,1)S(1)} %broadcast_in_dim.70, s32[]{:T(128)S(6)} %select_n.179, f32[256,512]{1,0:T(8,128)S(1)} %copy-done.9, ...), kind=kLoop, calls=%fused_computation.97 | loop fusion | flops 1310720 | bytes 3147780 | tf_op jit(solution)/shard_map/dynamic_update_slice | solution.py:29
  71.8 0.5 collective-permute-start.25
  72.7 1.6 %collective-permute-start.28 = (bf16[256,512]{1,0:T(8,128)(2,1)S(1)}, bf16[256,512]{1,0:T(8,128)(2,1)S(1)}, u32[]{:S(2)}, u32[]{:S(2)}) collective-permute-start(bf16[256,512]{1,0:T(8,128)(2,1)S(1)} %get-tuple-element.37), channel_id=1, source_target_pairs={{0,16},{8,24},{16,0},{24,8},{1,17},{9,25},{17,1},{25,9},{2,18},{10... | collective-permute-start | bytes 786440 | tf_op jit(solution)/shard_map/ppermute | solution.py:56
  74.4 0.6 collective-permute-start.14
  75.0 6.0 %collective-permute-done.25 = bf16[512,256]{1,0:T(8,128)(2,1)S(1)} collective-permute-done((bf16[512,256]{1,0:T(8,128)(2,1)S(1)}, bf16[512,256]{1,0:T(8,128)(2,1)S(1)}, u32[]{:S(2)}, u32[]{:S(2)}) %collective-permute-start.25) | collective-permute-done | bytes 262176 | tf_op jit(solution)/shard_map/ppermute | solution.py:56
  81.0 5.1 %collective-permute-done.28 = bf16[256,512]{1,0:T(8,128)(2,1)S(1)} collective-permute-done((bf16[256,512]{1,0:T(8,128)(2,1)S(1)}, bf16[256,512]{1,0:T(8,128)(2,1)S(1)}, u32[]{:S(2)}, u32[]{:S(2)}) %collective-permute-start.28) | collective-permute-done | bytes 262176 | tf_op jit(solution)/shard_map/ppermute | solution.py:56
  86.4 1.3 %collective-permute-done.29 = bf16[256,512]{1,0:T(8,128)(2,1)S(1)} collective-permute-done((bf16[256,512]{1,0:T(8,128)(2,1)S(1)}, bf16[256,512]{1,0:T(8,128)(2,1)S(1)}, u32[]{:S(2)}, u32[]{:S(2)}) %collective-permute-start.29) | collective-permute-done | bytes 262176 | tf_op jit(solution)/shard_map/ppermute | solution.py:50
  87.9 0.8 copy-done.10
  (126 shorter events, 4.1 us)
Async XLA Ops:
  0.7 7.0 %copy-start = (f32[1,2048,256]{2,1,0:T(8,128)S(1)}, f32[1,2048,256]{2,1,0:T(8,128)}, u32[]{:S(2)}) copy-start(f32[1,2048,256]{2,1,0:T(8,128)} %param.19) | copy-start | bytes 6291460
  2.3 20.8 %collective-permute-start.30 = (f32[6144]{0:T(1024)S(1)}, f32[6144]{0:T(1024)S(1)}, u32[]{:S(2)}, u32[]{:S(2)}) collective-permute-start(f32[6144]{0:T(1024)S(1)} %pad_maximum_fusion), channel_id=1, source_target_pairs={{0,16},{8,24},{16,0},{24,8},{1,17},{9,25},{17,1},{25,9},{2,18},{10... | collective-permute-start | bytes 73736 | tf_op jit(solution)/shard_map/ppermute | solution.py:56
  7.6 5.7 %collective-permute-start.1 = (f32[512,256]{1,0:T(8,128)}, f32[512,256]{1,0:T(8,128)S(1)}, u32[]{:S(2)}, u32[]{:S(2)}) collective-permute-start(f32[512,256]{1,0:T(8,128)} %get-tuple-element.67), channel_id=1, source_target_pairs={{0,8},{8,0},{16,24},{24,16},{1,9},{9,1},{17,25},{25,17},{2,10},{10... | collective-permute-start | bytes 1572872 | tf_op jit(solution)/shard_map/ppermute | solution.py:50
  8.7 6.0 %collective-permute-start.4 = (f32[512,256]{1,0:T(8,128)}, f32[512,256]{1,0:T(8,128)S(1)}, u32[]{:S(2)}, u32[]{:S(2)}) collective-permute-start(f32[512,256]{1,0:T(8,128)} %get-tuple-element.65), channel_id=1, source_target_pairs={{0,8},{8,0},{16,24},{24,16},{1,9},{9,1},{17,25},{25,17},{2,10},{10... | collective-permute-start | bytes 1572872 | tf_op jit(solution)/shard_map/ppermute | solution.py:50
  9.2 2.4 %copy-start.1 = (f32[1,2048,256]{2,1,0:T(8,128)S(1)}, f32[1,2048,256]{2,1,0:T(8,128)}, u32[]{:S(2)}) copy-start(f32[1,2048,256]{2,1,0:T(8,128)} %param.20) | copy-start | bytes 6291460
  11.6 41.9 %collective-permute-start.18 = (f32[256,512]{1,0:T(8,128)}, f32[256,512]{1,0:T(8,128)}, u32[]{:S(2)}, u32[]{:S(2)}) collective-permute-start(f32[256,512]{1,0:T(8,128)} %get-tuple-element.60), channel_id=1, source_target_pairs={{0,8},{8,0},{16,24},{24,16},{1,9},{9,1},{17,25},{25,17},{2,10},{10... | collective-permute-start | bytes 1572872 | tf_op jit(solution)/shard_map/ppermute | solution.py:50
  12.6 5.2 %collective-permute-start.16 = (f32[512,256]{1,0:T(8,128)}, f32[512,256]{1,0:T(8,128)}, u32[]{:S(2)}, u32[]{:S(2)}) collective-permute-start(f32[512,256]{1,0:T(8,128)} %get-tuple-element.63), channel_id=1, source_target_pairs={{0,8},{8,0},{16,24},{24,16},{1,9},{9,1},{17,25},{25,17},{2,10},{10... | collective-permute-start | bytes 1572872 | tf_op jit(solution)/shard_map/ppermute | solution.py:50
  13.3 6.7 %collective-permute-start.19 = (f32[256,512]{1,0:T(8,128)}, f32[256,512]{1,0:T(8,128)S(1)}, u32[]{:S(2)}, u32[]{:S(2)}) collective-permute-start(f32[256,512]{1,0:T(8,128)} %get-tuple-element.61), channel_id=1, source_target_pairs={{0,8},{8,0},{16,24},{24,16},{1,9},{9,1},{17,25},{25,17},{2,10},{10... | collective-permute-start | bytes 1572872 | tf_op jit(solution)/shard_map/ppermute | solution.py:50
  14.7 12.5 %copy-start.2 = (f32[512,256]{1,0:T(8,128)S(1)}, f32[512,256]{1,0:T(8,128)}, u32[]{:S(2)}) copy-start(f32[512,256]{1,0:T(8,128)} %param.24) | copy-start | bytes 1572868
  15.5 16.8 %copy-start.4 = (f32[512,256]{1,0:T(8,128)S(1)}, f32[512,256]{1,0:T(8,128)}, u32[]{:S(2)}) copy-start(f32[512,256]{1,0:T(8,128)} %param.25) | copy-start | bytes 1572868
  15.5 17.0 %collective-permute-start = (f32[512,256]{1,0:T(8,128)}, f32[512,256]{1,0:T(8,128)}, u32[]{:S(2)}, u32[]{:S(2)}) collective-permute-start(f32[512,256]{1,0:T(8,128)} %get-tuple-element.66), channel_id=1, source_target_pairs={{0,8},{8,0},{16,24},{24,16},{1,9},{9,1},{17,25},{25,17},{2,10},{10... | collective-permute-start | bytes 1572872 | tf_op jit(solution)/shard_map/ppermute | solution.py:50
  17.8 14.6 %copy-start.19 = (f32[1,2048]{1,0:T(1,128)S(1)}, f32[1,2048]{1,0:T(1,128)}, u32[]{:S(2)}) copy-start(f32[1,2048]{1,0:T(1,128)} %param.23) | copy-start | bytes 24580
  17.8 14.6 %copy-start.20 = (f32[1,2048]{1,0:T(1,128)S(1)}, f32[1,2048]{1,0:T(1,128)}, u32[]{:S(2)}) copy-start(f32[1,2048]{1,0:T(1,128)} %param.22) | copy-start | bytes 24580
  17.8 9.3 %collective-permute-start.2 = (f16[512,256]{1,0:T(8,128)(2,1)S(1)}, f16[512,256]{1,0:T(8,128)(2,1)}, u32[]{:S(2)}, u32[]{:S(2)}) collective-permute-start(f16[512,256]{1,0:T(8,128)(2,1)S(1)} %multiply_convert_fusion.3), channel_id=1, source_target_pairs={{0,16},{8,24},{16,0},{24,8},{1,17},{9,25},{17,1},{25,9},{2,18},{10... | collective-permute-start | bytes 786440 | tf_op jit(solution)/shard_map/ppermute | solution.py:56
  20.0 11.9 %collective-permute-start.5 = (f16[512,256]{1,0:T(8,128)(2,1)}, f16[512,256]{1,0:T(8,128)(2,1)}, u32[]{:S(2)}, u32[]{:S(2)}) collective-permute-start(f16[512,256]{1,0:T(8,128)(2,1)} %multiply_convert_fusion.2), channel_id=1, source_target_pairs={{0,16},{8,24},{16,0},{24,8},{1,17},{9,25},{17,1},{25,9},{2,18},{10... | collective-permute-start | bytes 786440 | tf_op jit(solution)/shard_map/ppermute | solution.py:56
  23.2 11.1 %collective-permute-start.3 = (f32[512,256]{1,0:T(8,128)}, f32[512,256]{1,0:T(8,128)}, u32[]{:S(2)}, u32[]{:S(2)}) collective-permute-start(f32[512,256]{1,0:T(8,128)} %get-tuple-element.64), channel_id=1, source_target_pairs={{0,8},{8,0},{16,24},{24,16},{1,9},{9,1},{17,25},{25,17},{2,10},{10... | collective-permute-start | bytes 1572872 | tf_op jit(solution)/shard_map/ppermute | solution.py:50
  27.2 18.5 %collective-permute-start.15 = (f32[512,256]{1,0:T(8,128)}, f32[512,256]{1,0:T(8,128)}, u32[]{:S(2)}, u32[]{:S(2)}) collective-permute-start(f32[512,256]{1,0:T(8,128)} %get-tuple-element.62), channel_id=1, source_target_pairs={{0,8},{8,0},{16,24},{24,16},{1,9},{9,1},{17,25},{25,17},{2,10},{10... | collective-permute-start | bytes 1572872 | tf_op jit(solution)/shard_map/ppermute | solution.py:50
  27.4 10.7 %copy-start.6 = (f32[512,256]{1,0:T(8,128)S(1)}, f32[512,256]{1,0:T(8,128)}, u32[]{:S(2)}) copy-start(f32[512,256]{1,0:T(8,128)} %param.26) | copy-start | bytes 1572868
  31.9 19.7 %collective-permute-start.20 = (f16[256,512]{1,0:T(8,128)(2,1)S(1)}, f16[256,512]{1,0:T(8,128)(2,1)}, u32[]{:S(2)}, u32[]{:S(2)}) collective-permute-start(f16[256,512]{1,0:T(8,128)(2,1)S(1)} %multiply_convert_fusion), channel_id=1, source_target_pairs={{0,16},{8,24},{16,0},{24,8},{1,17},{9,25},{17,1},{25,9},{2,18},{10... | collective-permute-start | bytes 786440 | tf_op jit(solution)/shard_map/ppermute | solution.py:56
  32.4 9.4 %copy-start.8 = (f32[256,512]{1,0:T(8,128)S(1)}, f32[256,512]{1,0:T(8,128)}, u32[]{:S(2)}) copy-start(f32[256,512]{1,0:T(8,128)} %param.27) | copy-start | bytes 1572868
  32.5 12.7 %collective-permute-start.17 = (f16[512,256]{1,0:T(8,128)(2,1)}, f16[512,256]{1,0:T(8,128)(2,1)}, u32[]{:S(2)}, u32[]{:S(2)}) collective-permute-start(f16[512,256]{1,0:T(8,128)(2,1)} %multiply_convert_fusion.1), channel_id=1, source_target_pairs={{0,16},{8,24},{16,0},{24,8},{1,17},{9,25},{17,1},{25,9},{2,18},{10... | collective-permute-start | bytes 786440 | tf_op jit(solution)/shard_map/ppermute | solution.py:56
  36.4 14.0 %copy-start.3 = (f32[512,256]{1,0:T(8,128)S(1)}, f32[512,256]{1,0:T(8,128)}, u32[]{:S(2)}) copy-start(f32[512,256]{1,0:T(8,128)} %param.24) | copy-start | bytes 1572868
  36.4 14.0 %copy-start.15 = (f32[512,256]{1,0:T(8,128)S(1)}, f32[512,256]{1,0:T(8,128)}, u32[]{:S(2)}) copy-start(f32[512,256]{1,0:T(8,128)} %param.30) | copy-start | bytes 1572868
  36.5 3.7 %collective-permute-start.6 = (f32[4,512]{1,0:T(4,128)S(1)}, f32[4,512]{1,0:T(4,128)S(1)}, u32[]{:S(2)}, u32[]{:S(2)}) collective-permute-start(f32[4,512]{1,0:T(4,128)S(1)} %pad_maximum_fusion.2), channel_id=1, source_target_pairs={{0,1},{1,0},{2,3},{3,2},{4,5},{5,4},{6,7},{7,6},{8,9},{9,8},{10,11... | collective-permute-start | bytes 24584 | tf_op jit(solution)/shard_map/ppermute | solution.py:143
  40.2 5.0 %collective-permute-start.7 = (f32[4,512]{1,0:T(4,128)S(1)}, f32[4,512]{1,0:T(4,128)S(1)}, u32[]{:S(2)}, u32[]{:S(2)}) collective-permute-start(f32[4,512]{1,0:T(4,128)S(1)} %fusion.42), channel_id=1, source_target_pairs={{0,2},{1,3},{2,0},{3,1},{4,6},{5,7},{6,4},{7,5},{8,10},{9,11},{10,... | collective-permute-start | bytes 24584 | tf_op jit(solution)/shard_map/ppermute | solution.py:143
  45.1 15.6 %collective-permute-start.32 = (f32[2,2048]{1,0:T(2,128)S(1)}, f32[2,2048]{1,0:T(2,128)S(1)}, u32[]{:S(2)}, u32[]{:S(2)}) collective-permute-start(f32[2,2048]{1,0:T(2,128)S(1)} %fusion.25), channel_id=1, source_target_pairs={{0,8},{8,0},{16,24},{24,16},{1,9},{9,1},{17,25},{25,17},{2,10},{10... | collective-permute-start | bytes 49160 | tf_op jit(solution)/shard_map/ppermute | solution.py:50
  45.2 10.3 %collective-permute-start.31 = (f32[4,4,512]{2,0,1:T(4,128)S(1)}, f32[4,4,512]{2,0,1:T(4,128)S(1)}, u32[]{:S(2)}, u32[]{:S(2)}) collective-permute-start(f32[4,4,512]{2,0,1:T(4,128)S(1)} %dynamic_update_slice.73), channel_id=1, source_target_pairs={{0,8},{8,0},{16,24},{24,16},{1,9},{9,1},{17,25},{25,17},{2,10},{10... | collective-permute-start | bytes 98312 | tf_op jit(solution)/shard_map/ppermute | solution.py:50
  45.7 4.6 %collective-permute-start.8 = (f32[4,512]{1,0:T(4,128)S(1)}, f32[4,512]{1,0:T(4,128)S(1)}, u32[]{:S(2)}, u32[]{:S(2)}) collective-permute-start(f32[4,512]{1,0:T(4,128)S(1)} %fusion.55), channel_id=1, source_target_pairs={{0,4},{1,5},{2,6},{3,7},{4,0},{5,1},{6,2},{7,3},{8,12},{9,13},{10,... | collective-permute-start | bytes 24584 | tf_op jit(solution)/shard_map/ppermute | solution.py:143
  50.4 1.8 %copy-start.5 = (f32[512,256]{1,0:T(8,128)S(1)}, f32[512,256]{1,0:T(8,128)}, u32[]{:S(2)}) copy-start(f32[512,256]{1,0:T(8,128)} %param.25) | copy-start | bytes 1572868
  50.5 1.8 %copy-start.16 = (f32[512,256]{1,0:T(8,128)S(1)}, f32[512,256]{1,0:T(8,128)}, u32[]{:S(2)}) copy-start(f32[512,256]{1,0:T(8,128)} %param.31) | copy-start | bytes 1572868
  51.7 20.1 %collective-permute-start.9 = (bf16[512,256]{1,0:T(8,128)(2,1)S(1)}, bf16[512,256]{1,0:T(8,128)(2,1)S(1)}, u32[]{:S(2)}, u32[]{:S(2)}) collective-permute-start(bf16[512,256]{1,0:T(8,128)(2,1)S(1)} %get-tuple-element.53), channel_id=1, source_target_pairs={{0,8},{8,0},{16,24},{24,16},{1,9},{9,1},{17,25},{25,17},{2,10},{10... | collective-permute-start | bytes 786440 | tf_op jit(solution)/shard_map/ppermute | solution.py:50
  51.7 20.6 %collective-permute-start.10 = (bf16[512,256]{1,0:T(8,128)(2,1)S(1)}, bf16[512,256]{1,0:T(8,128)(2,1)S(1)}, u32[]{:S(2)}, u32[]{:S(2)}) collective-permute-start(bf16[512,256]{1,0:T(8,128)(2,1)S(1)} %get-tuple-element.53), channel_id=1, source_target_pairs={{0,16},{8,24},{16,0},{24,8},{1,17},{9,25},{17,1},{25,9},{2,18},{10... | collective-permute-start | bytes 786440 | tf_op jit(solution)/shard_map/ppermute | solution.py:56
  53.5 15.7 %copy-start.7 = (f32[512,256]{1,0:T(8,128)S(1)}, f32[512,256]{1,0:T(8,128)}, u32[]{:S(2)}) copy-start(f32[512,256]{1,0:T(8,128)} %param.26) | copy-start | bytes 1572868
  53.5 15.7 %copy-start.17 = (f32[512,256]{1,0:T(8,128)S(1)}, f32[512,256]{1,0:T(8,128)}, u32[]{:S(2)}) copy-start(f32[512,256]{1,0:T(8,128)} %param.32) | copy-start | bytes 1572868
  53.5 19.2 %collective-permute-start.12 = (bf16[512,256]{1,0:T(8,128)(2,1)S(1)}, bf16[512,256]{1,0:T(8,128)(2,1)S(1)}, u32[]{:S(2)}, u32[]{:S(2)}) collective-permute-start(bf16[512,256]{1,0:T(8,128)(2,1)S(1)} %get-tuple-element.49), channel_id=1, source_target_pairs={{0,8},{8,0},{16,24},{24,16},{1,9},{9,1},{17,25},{25,17},{2,10},{10... | collective-permute-start | bytes 786440 | tf_op jit(solution)/shard_map/ppermute | solution.py:50
  55.4 3.7 %collective-permute-start.21 = (f32[4,512]{1,0:T(4,128)S(1)}, f32[4,512]{1,0:T(4,128)S(1)}, u32[]{:S(2)}, u32[]{:S(2)}) collective-permute-start(f32[4,512]{1,0:T(4,128)S(1)} %pad_maximum_fusion.3), channel_id=1, source_target_pairs={{0,1},{1,0},{2,3},{3,2},{4,5},{5,4},{6,7},{7,6},{8,9},{9,8},{10,11... | collective-permute-start | bytes 24584 | tf_op jit(solution)/shard_map/ppermute | solution.py:143
  59.1 15.2 %collective-permute-start.13 = (bf16[512,256]{1,0:T(8,128)(2,1)S(1)}, bf16[512,256]{1,0:T(8,128)(2,1)S(1)}, u32[]{:S(2)}, u32[]{:S(2)}) collective-permute-start(bf16[512,256]{1,0:T(8,128)(2,1)S(1)} %get-tuple-element.49), channel_id=1, source_target_pairs={{0,16},{8,24},{16,0},{24,8},{1,17},{9,25},{17,1},{25,9},{2,18},{10... | collective-permute-start | bytes 786440 | tf_op jit(solution)/shard_map/ppermute | solution.py:56
  60.7 3.7 %collective-permute-start.22 = (f32[4,512]{1,0:T(4,128)S(1)}, f32[4,512]{1,0:T(4,128)S(1)}, u32[]{:S(2)}, u32[]{:S(2)}) collective-permute-start(f32[4,512]{1,0:T(4,128)S(1)} %fusion.41), channel_id=1, source_target_pairs={{0,2},{1,3},{2,0},{3,1},{4,6},{5,7},{6,4},{7,5},{8,10},{9,11},{10,... | collective-permute-start | bytes 24584 | tf_op jit(solution)/shard_map/ppermute | solution.py:143
  64.5 4.6 %collective-permute-start.23 = (f32[4,512]{1,0:T(4,128)S(1)}, f32[4,512]{1,0:T(4,128)S(1)}, u32[]{:S(2)}, u32[]{:S(2)}) collective-permute-start(f32[4,512]{1,0:T(4,128)S(1)} %fusion.54), channel_id=1, source_target_pairs={{0,4},{1,5},{2,6},{3,7},{4,0},{5,1},{6,2},{7,3},{8,12},{9,13},{10,... | collective-permute-start | bytes 24584 | tf_op jit(solution)/shard_map/ppermute | solution.py:143
  70.5 4.0 %collective-permute-start.24 = (bf16[512,256]{1,0:T(8,128)(2,1)S(1)}, bf16[512,256]{1,0:T(8,128)(2,1)S(1)}, u32[]{:S(2)}, u32[]{:S(2)}) collective-permute-start(bf16[512,256]{1,0:T(8,128)(2,1)S(1)} %get-tuple-element.41), channel_id=1, source_target_pairs={{0,8},{8,0},{16,24},{24,16},{1,9},{9,1},{17,25},{25,17},{2,10},{10... | collective-permute-start | bytes 786440 | tf_op jit(solution)/shard_map/ppermute | solution.py:50
  71.8 9.2 %collective-permute-start.25 = (bf16[512,256]{1,0:T(8,128)(2,1)S(1)}, bf16[512,256]{1,0:T(8,128)(2,1)S(1)}, u32[]{:S(2)}, u32[]{:S(2)}) collective-permute-start(bf16[512,256]{1,0:T(8,128)(2,1)S(1)} %get-tuple-element.41), channel_id=1, source_target_pairs={{0,16},{8,24},{16,0},{24,8},{1,17},{9,25},{17,1},{25,9},{2,18},{10... | collective-permute-start | bytes 786440 | tf_op jit(solution)/shard_map/ppermute | solution.py:56
  72.3 13.8 %collective-permute-start.27 = (bf16[256,512]{1,0:T(8,128)(2,1)S(1)}, bf16[256,512]{1,0:T(8,128)(2,1)S(1)}, u32[]{:S(2)}, u32[]{:S(2)}) collective-permute-start(bf16[256,512]{1,0:T(8,128)(2,1)S(1)} %get-tuple-element.37), channel_id=1, source_target_pairs={{0,8},{8,0},{16,24},{24,16},{1,9},{9,1},{17,25},{25,17},{2,10},{10... | collective-permute-start | bytes 786440 | tf_op jit(solution)/shard_map/ppermute | solution.py:50
  72.7 13.5 %collective-permute-start.28 = (bf16[256,512]{1,0:T(8,128)(2,1)S(1)}, bf16[256,512]{1,0:T(8,128)(2,1)S(1)}, u32[]{:S(2)}, u32[]{:S(2)}) collective-permute-start(bf16[256,512]{1,0:T(8,128)(2,1)S(1)} %get-tuple-element.37), channel_id=1, source_target_pairs={{0,16},{8,24},{16,0},{24,8},{1,17},{9,25},{17,1},{25,9},{2,18},{10... | collective-permute-start | bytes 786440 | tf_op jit(solution)/shard_map/ppermute | solution.py:56
  74.3 11.9 %collective-permute-start.11 = (bf16[512,256]{1,0:T(8,128)(2,1)S(1)}, bf16[512,256]{1,0:T(8,128)(2,1)S(1)}, u32[]{:S(2)}, u32[]{:S(2)}) collective-permute-start(bf16[512,256]{1,0:T(8,128)(2,1)S(1)} %collective-permute-done.10), channel_id=1, source_target_pairs={{0,8},{8,0},{16,24},{24,16},{1,9},{9,1},{17,25},{25,17},{2,10},{10... | collective-permute-start | bytes 786440 | tf_op jit(solution)/shard_map/ppermute | solution.py:50
  74.4 11.9 %collective-permute-start.14 = (bf16[512,256]{1,0:T(8,128)(2,1)S(1)}, bf16[512,256]{1,0:T(8,128)(2,1)S(1)}, u32[]{:S(2)}, u32[]{:S(2)}) collective-permute-start(bf16[512,256]{1,0:T(8,128)(2,1)S(1)} %collective-permute-done.13), channel_id=1, source_target_pairs={{0,8},{8,0},{16,24},{24,16},{1,9},{9,1},{17,25},{25,17},{2,10},{10... | collective-permute-start | bytes 786440 | tf_op jit(solution)/shard_map/ppermute | solution.py:50
  81.0 5.4 %collective-permute-start.26 = (bf16[512,256]{1,0:T(8,128)(2,1)S(1)}, bf16[512,256]{1,0:T(8,128)(2,1)S(1)}, u32[]{:S(2)}, u32[]{:S(2)}) collective-permute-start(bf16[512,256]{1,0:T(8,128)(2,1)S(1)} %collective-permute-done.25), channel_id=1, source_target_pairs={{0,8},{8,0},{16,24},{24,16},{1,9},{9,1},{17,25},{25,17},{2,10},{10... | collective-permute-start | bytes 786440 | tf_op jit(solution)/shard_map/ppermute | solution.py:50
  86.2 1.5 %collective-permute-start.29 = (bf16[256,512]{1,0:T(8,128)(2,1)S(1)}, bf16[256,512]{1,0:T(8,128)(2,1)S(1)}, u32[]{:S(2)}, u32[]{:S(2)}) collective-permute-start(bf16[256,512]{1,0:T(8,128)(2,1)S(1)} %collective-permute-done.28), channel_id=1, source_target_pairs={{0,8},{8,0},{16,24},{24,16},{1,9},{9,1},{17,25},{25,17},{2,10},{10... | collective-permute-start | bytes 786440 | tf_op jit(solution)/shard_map/ppermute | solution.py:50
  86.4 1.6 %copy-start.11 = (bf16[4,512,256]{2,1,0:T(8,128)(2,1)}, bf16[4,512,256]{2,1,0:T(8,128)(2,1)S(1)}, u32[]{:S(2)}) copy-start(bf16[4,512,256]{2,1,0:T(8,128)(2,1)S(1)} %bitcast_dynamic-update-slice_fusion) | copy-start | bytes 3145732
  (6 other events, 7.4 us)

commit v2 on v1

--- a/solution.py
+++ b/solution.py
@@ -7,8 +7,8 @@
 learn_rate = 0.015
 hold_rate = 0.8
 
-half_bound = 8.0
-wire_scale = 60000.0 / half_bound**1.5
+code_scale = 200.0
+code_power = 12
 
 
 names = ("query", "key", "value", "mixed")
@@ -59,24 +59,31 @@
         return lax.optimization_barrier((value, *others))[0]
 
     def encode(value):
-        size = jnp.abs(value)
-        root = size * lax.rsqrt(jnp.maximum(size, 1e-30))
-        return (value * root * wire_scale).astype(jnp.float16)
+        value = value * code_scale
+        cube = value * value * value
+        size = (cube * cube) * (cube * cube)
+        return jnp.where(value < 0, -size, size).astype(jnp.bfloat16)
 
     def decode(code):
         code = code.astype(jnp.float32)
-        size = jnp.exp(jnp.log(jnp.abs(code) * (1.0 / wire_scale)) * (2.0 / 3.0))
+        size = jnp.exp(jnp.log(jnp.abs(code)) * (1.0 / code_power)) * (1.0 / code_scale)
         return jnp.where(code < 0, -size, size)
 
     def other(step):
         return (chip + step) % chips * width + core
+
+    early = "query"
 
     def paired(n, step):
         own = block_of(partial[n], other(step), count, axis_of[n])
         if width == 1:
             return own
-        theirs = block_of(partial[n], other(step) ^ 1, count, axis_of[n])
-        return own + to_pair(theirs)
+        if n == early and step == 1:
+            theirs = block_of(partial[n], other(step) ^ 1, count, axis_of[n])
+            return own + to_pair(theirs)
+        return own + block_of(crossed[n], other(step), count, axis_of[n])
+
+    crossed = {n: to_pair(partial[n]) for n in names} if width == 2 else {}
 
     own_vectors = jnp.concatenate([master_vectors, memory_vectors])
     vector_sum, vector_all = partial_vectors, jnp.zeros((count,) + own_vectors.shape, jnp.float32)
@@ -89,7 +96,8 @@
     for n in names:
         arrived[n] = []
         for step in range(1, chips):
-            arrived[n].append(to_chip(encode(paired(n, step)), step))
+            code = encode(paired(n, step))
+            arrived[n].append(to_chip(code, step))
 
     for step, got in enumerate(vector_got, 1):
         got = after(got, *arrived["query"])
@@ -103,7 +111,7 @@
 
     mean, outs = {}, {}
 
-    def reduce(n, *others):
+    def reduce_in(n, *others):
         total = paired(n, 0)
         for piece in arrived[n]:
             total = total + decode(after(piece, *others))
@@ -146,11 +154,11 @@
             bit *= 2
         return found
 
-    slope_q = reduce("query")
-    slope_k = reduce("key")
+    slope_q = reduce_in("query")
+    slope_k = reduce_in("key")
     first = stages(jnp.stack([own_size("query"), own_size("key"), slope_q, slope_k]))
-    slope_v = reduce("value", first[0])
-    slope_m = reduce("mixed", first[-1])
+    slope_v = reduce_in("value", first[0])
+    slope_m = reduce_in("mixed", first[-1])
     second = stages(jnp.stack([own_size("value"), own_size("mixed"), slope_v, slope_m]))
     total = first[-1]
     finish("query", total[0], total[2])

time: 89.1 us -> 86.4 us (0.970)
  waiting for transfers between devices: 31.2 us -> 38.4 us
  local copies, waits for them, and re-layouts: 10.7 us -> 4.65 us
  other arithmetic: 19.1 us -> 16.5 us
  starting transfers between devices: 26.5 us -> 25.1 us
    ppermute x9, waiting for transfers between devices: 22.8 us -> 29.1 us  [to_chip(): return lax.ppermute(value, 'replica', pairs)]
    ppermute x18 -> x15, waiting for transfers between devices: 1.34 us -> 5.27 us  [to_pair(): return lax.ppermute(value, 'replica', [(i, i ^ 1) for i in range(count)])]
    squeeze x3 -> x1, local copies, waits for them, and re-layouts: 4.33 us -> 1.21 us  [block_of(): return lax.dynamic_index_in_dim(split, index, axis=0, keepdims=False)]
    ppermute x6, waiting for transfers between devices: 7.1 us -> 4 us  [stages(): got = lax.ppermute(value, 'model', [(i, i ^ bit) for i in range(models)])]
    dynamic_slice x1 -> x0, local copies, waits for them, and re-layouts: 2.38 us -> none  [block_of(): return lax.dynamic_slice_in_dim(whole, index * size, size, axis=1)]
    convert_element_type x4, other arithmetic: 6.37 us -> 5.01 us  [encode(): return jnp.where(value < 0, -size, size).astype(jnp.bfloat16)]
    ppermute x6, starting transfers between devices: 11.7 us -> 10.7 us  [stages(): got = lax.ppermute(value, 'model', [(i, i ^ bit) for i in range(models)])]
    ppermute x18 -> x15, starting transfers between devices: 3.4 us -> 2.69 us  [to_pair(): return lax.ppermute(value, 'replica', [(i, i ^ 1) for i in range(count)])]
  transfers between devices with their start and end apart: 33 -> 30, of which waited for: 11 -> 11; matrix products, arithmetic and copies ran while one was open for 30% -> 20% of each run, Pallas kernels for 0% -> 0%
where the time goes in v2:
time: 86.4 us; the launch traced here: 86 us
  waiting for transfers between devices  38.4 us (44%)
  starting transfers between devices  25.1 us (29%)
  other arithmetic  16.5 us (19%)
  local copies, waits for them, and re-layouts  4.65 us (5%)
  between operations  1.35 us (2%)
    ppermute x9, waiting for transfers between devices, to_chip(): return lax.ppermute(value, 'replica', pairs)  29.1 us
    ppermute x9, starting transfers between devices, to_chip(): return lax.ppermute(value, 'replica', pairs)  11.7 us
    ppermute x6, starting transfers between devices, stages(): got = lax.ppermute(value, 'model', [(i, i ^ bit) for i in range(models)])  10.7 us
    ppermute x15, waiting for transfers between devices, to_pair(): return lax.ppermute(value, 'replica', [(i, i ^ 1) for i in range(count)])  5.27 us
    reduce_sum x3, other arithmetic, reduce_in(): return jnp.sum(mean[n] * mean[n], axis=1 - axis_of[n])  5.04 us
    convert_element_type x4, other arithmetic, encode(): return jnp.where(value < 0, -size, size).astype(jnp.bfloat16)  5.01 us
    ppermute x6, waiting for transfers between devices, stages(): got = lax.ppermute(value, 'model', [(i, i ^ bit) for i in range(models)])  4 us
    dynamic_update_slice x3, other arithmetic, put_block(): lax.dynamic_update_index_in_dim(split, block[None], index, axis=0)  3.68 us
  transfers between devices with their start and end apart: 30, of which 11 were waited for; matrix products, arithmetic and copies ran while one was open for 20% of the time, Pallas kernels for 0%

profile of v2, /device:TPU:0, one launch (start us, length us, event | category | flops | bytes accessed | tf_op | source)
XLA Modules:
  0.0 86.0 jit_solution(17795448485330584964)
XLA Ops:
  0.8 1.2 %dynamic-slice_bitcast_fusion = f32[512,256]{1,0:T(8,128)S(1)} fusion(f32[4,512,256]{2,1,0:T(8,128)} %bitcast.110, s32[]{:T(128)S(6)} %select_n.170), kind=kLoop, calls=%fused_computation.79 | loop fusion | bytes 1048580 | tf_op jit(solution)/shard_map/jit(dynamic_index_in_dim)/squeeze | solution.py:20
  2.0 0.6 collective-permute-start.1
  2.7 0.7 fusion.40
  3.4 0.7 collective-permute-done.1
  4.1 1.2 %fusion.18 = bf16[512,256]{1,0:T(8,128)(2,1)S(1)} fusion(f32[512,256]{1,0:T(8,128)S(1)} %collective-permute-done.1, f32[4,512,256]{2,1,0:T(8,128)} %bitcast.111, s32[]{:T(128)S(6)} %select_n.169), kind=kLoop, calls=%fused_computation.42 | loop fusion | flops 1310720 | bytes 1310724 | tf_op jit(solution)/shard_map/convert_element_type | solution.py:65
  5.3 2.9 %collective-permute-start.2 = (bf16[512,256]{1,0:T(8,128)(2,1)S(1)}, bf16[512,256]{1,0:T(8,128)(2,1)S(1)}, u32[]{:S(2)}, u32[]{:S(2)}) collective-permute-start(bf16[512,256]{1,0:T(8,128)(2,1)S(1)} %fusion.18), channel_id=1, source_target_pairs={{0,16},{8,24},{16,0},{24,8},{1,17},{9,25},{17,1},{25,9},{2,18},{10... | collective-permute-start | bytes 786440 | tf_op jit(solution)/shard_map/ppermute | solution.py:56
  8.5 0.5 collective-permute-start.16
  9.2 6.3 %collective-permute-done.27 = f32[6144]{0:T(1024)S(1)} collective-permute-done((f32[6144]{0:T(1024)S(1)}, f32[6144]{0:T(1024)S(1)}, u32[]{:S(2)}, u32[]{:S(2)}) %collective-permute-start.27) | collective-permute-done | bytes 24608 | tf_op jit(solution)/shard_map/ppermute | solution.py:56
  15.5 0.6 collective-permute-start.28
  16.2 0.1 multiply_reduce_fusion.6
  16.7 3.2 %collective-permute-done.28 = f32[4,4,512]{2,0,1:T(4,128)S(1)} collective-permute-done((f32[4,4,512]{2,0,1:T(4,128)S(1)}, f32[4,4,512]{2,0,1:T(4,128)S(1)}, u32[]{:S(2)}, u32[]{:S(2)}) %collective-permute-start.28) | collective-permute-done | bytes 32800 | tf_op jit(solution)/shard_map/ppermute | solution.py:50
  20.2 1.4 %fusion.22 = bf16[512,256]{1,0:T(8,128)(2,1)S(1)} fusion(f32[4,512,256]{2,1,0:T(8,128)} %bitcast.11, s32[]{:T(128)S(6)} %select_n.169, f32[4,512,256]{2,1,0:T(8,128)} %bitcast.118), kind=kLoop, calls=%fused_computation.46 | loop fusion | flops 1310720 | bytes 1310724 | tf_op jit(solution)/shard_map/convert_element_type | solution.py:65
  21.6 1.8 %collective-permute-start.4 = (bf16[512,256]{1,0:T(8,128)(2,1)S(1)}, bf16[512,256]{1,0:T(8,128)(2,1)S(1)}, u32[]{:S(2)}, u32[]{:S(2)}) collective-permute-start(bf16[512,256]{1,0:T(8,128)(2,1)S(1)} %fusion.22), channel_id=1, source_target_pairs={{0,16},{8,24},{16,0},{24,8},{1,17},{9,25},{17,1},{25,9},{2,18},{10... | collective-permute-start | bytes 786440 | tf_op jit(solution)/shard_map/ppermute | solution.py:56
  23.4 0.7 fusion.66
  24.1 0.6 slice_reduce_fusion
  24.7 5.5 %collective-permute-done.4 = bf16[512,256]{1,0:T(8,128)(2,1)S(1)} collective-permute-done((bf16[512,256]{1,0:T(8,128)(2,1)S(1)}, bf16[512,256]{1,0:T(8,128)(2,1)S(1)}, u32[]{:S(2)}, u32[]{:S(2)}) %collective-permute-start.4) | collective-permute-done | bytes 262176 | tf_op jit(solution)/shard_map/ppermute | solution.py:56
  30.2 2.3 %multiply_reduce_fusion.4 = (f32[512]{0:T(512)S(1)}, f32[512,256]{1,0:T(8,128)S(1)}, f32[512]{0:T(512)S(1)}, f32[512,256]{1,0:T(8,128)S(1)}) fusion(bf16[512,256]{1,0:T(8,128)(2,1)S(1)} %collective-permute-done.4, f32[4,512,256]{2,1,0:T(8,128)} %bitcast.11, s32[]{:T(128)S(6)} %select_n.167, f32[4,512,256]{2,1,0:T(8,128)} %bitcast.119, ...), kind=kLoop, calls=%fused_computation.75 | loop fusion | flops 3144704 | bytes 3674116 | tf_op jit(solution)/shard_map/reduce_sum | solution.py:119
  32.5 1.8 %collective-permute-start.5 = (f32[4,512]{1,0:T(4,128)S(1)}, f32[4,512]{1,0:T(4,128)S(1)}, u32[]{:S(2)}, u32[]{:S(2)}) collective-permute-start(f32[4,512]{1,0:T(4,128)S(1)} %pad_maximum_fusion.2), channel_id=1, source_target_pairs={{0,1},{1,0},{2,3},{3,2},{4,5},{5,4},{6,7},{7,6},{8,9},{9,8},{10,11... | collective-permute-start | bytes 24584 | tf_op jit(solution)/shard_map/ppermute | solution.py:151
  34.3 1.2 %fusion.28 = bf16[512,256]{1,0:T(8,128)(2,1)S(1)} fusion(f32[4,512,256]{2,1,0:T(8,128)} %bitcast.29, s32[]{:T(128)S(6)} %select_n.169, f32[4,512,256]{2,1,0:T(8,128)S(1)} %bitcast.121), kind=kLoop, calls=%fused_computation.52 | loop fusion | flops 1310720 | bytes 1310724 | tf_op jit(solution)/shard_map/convert_element_type | solution.py:65
  35.5 1.6 %collective-permute-start.15 = (bf16[512,256]{1,0:T(8,128)(2,1)S(1)}, bf16[512,256]{1,0:T(8,128)(2,1)S(1)}, u32[]{:S(2)}, u32[]{:S(2)}) collective-permute-start(bf16[512,256]{1,0:T(8,128)(2,1)S(1)} %fusion.28), channel_id=1, source_target_pairs={{0,16},{8,24},{16,0},{24,8},{1,17},{9,25},{17,1},{25,9},{2,18},{10... | collective-permute-start | bytes 786440 | tf_op jit(solution)/shard_map/ppermute | solution.py:56
  37.1 1.6 %collective-permute-start.6 = (f32[4,512]{1,0:T(4,128)S(1)}, f32[4,512]{1,0:T(4,128)S(1)}, u32[]{:S(2)}, u32[]{:S(2)}) collective-permute-start(f32[4,512]{1,0:T(4,128)S(1)} %fusion.56), channel_id=1, source_target_pairs={{0,2},{1,3},{2,0},{3,1},{4,6},{5,7},{6,4},{7,5},{8,10},{9,11},{10,... | collective-permute-start | bytes 24584 | tf_op jit(solution)/shard_map/ppermute | solution.py:151
  38.8 1.2 %fusion.32 = bf16[256,512]{1,0:T(8,128)(2,1)S(1)} fusion(f32[256,2048]{1,0:T(8,128)} %collective-permute-done.16, s32[]{:T(128)S(6)} %select_n.183, f32[1,256,2048]{2,1,0:T(8,128)S(1)} %copy-done.9), kind=kLoop, calls=%fused_computation.56 | loop fusion | flops 1310720 | bytes 1310724 | tf_op jit(solution)/shard_map/convert_element_type | solution.py:65
  40.0 0.9 %collective-permute-start.17 = (bf16[256,512]{1,0:T(8,128)(2,1)S(1)}, bf16[256,512]{1,0:T(8,128)(2,1)S(1)}, u32[]{:S(2)}, u32[]{:S(2)}) collective-permute-start(bf16[256,512]{1,0:T(8,128)(2,1)S(1)} %fusion.32), channel_id=1, source_target_pairs={{0,16},{8,24},{16,0},{24,8},{1,17},{9,25},{17,1},{25,9},{2,18},{10... | collective-permute-start | bytes 786440 | tf_op jit(solution)/shard_map/ppermute | solution.py:56
  40.9 3.8 %collective-permute-done.15 = bf16[512,256]{1,0:T(8,128)(2,1)S(1)} collective-permute-done((bf16[512,256]{1,0:T(8,128)(2,1)S(1)}, bf16[512,256]{1,0:T(8,128)(2,1)S(1)}, u32[]{:S(2)}, u32[]{:S(2)}) %collective-permute-start.15) | collective-permute-done | bytes 262176 | tf_op jit(solution)/shard_map/ppermute | solution.py:56
  44.8 2.7 %collective-permute-start.7 = (f32[4,512]{1,0:T(4,128)S(1)}, f32[4,512]{1,0:T(4,128)S(1)}, u32[]{:S(2)}, u32[]{:S(2)}) collective-permute-start(f32[4,512]{1,0:T(4,128)S(1)} %fusion.69), channel_id=1, source_target_pairs={{0,4},{1,5},{2,6},{3,7},{4,0},{5,1},{6,2},{7,3},{8,12},{9,13},{10,... | collective-permute-start | bytes 24584 | tf_op jit(solution)/shard_map/ppermute | solution.py:151
  47.4 1.4 %multiply_reduce_fusion.1 = (f32[512]{0:T(512)S(1)}, f32[512,256]{1,0:T(8,128)S(1)}) fusion(bf16[512,256]{1,0:T(8,128)(2,1)S(1)} %collective-permute-done.15, f32[4,512,256]{2,1,0:T(8,128)} %bitcast.29, s32[]{:T(128)S(6)} %select_n.167, f32[4,512,256]{2,1,0:T(8,128)S(1)} %bitcast.122), kind=kLoop, calls=%fused_computation.70 | loop fusion | flops 1572352 | bytes 1837060 | tf_op jit(solution)/shard_map/reduce_sum | solution.py:119
  48.8 0.6 collective-permute-done.7
  49.4 1.3 %multiply_reduce_fusion = (f32[512]{0:T(512)S(1)}, f32[256,512]{1,0:T(8,128)S(1)}) fusion(bf16[256,512]{1,0:T(8,128)(2,1)S(1)} %collective-permute-done.17, f32[256,2048]{1,0:T(8,128)} %collective-permute-done.16, s32[]{:T(128)S(6)} %select_n.182, f32[1,256,2048]{2,1,0:T(8,128)S(1)} %copy-done.9), kind=kLoop, calls=%fused_computation.69 | loop fusion | flops 1572352 | bytes 1837060 | tf_op jit(solution)/shard_map/reduce_sum | solution.py:119
  50.8 0.3 collective-permute-start.18
  51.1 3.4 %collective-permute-done.18 = f32[4,512]{1,0:T(4,128)S(1)} collective-permute-done((f32[4,512]{1,0:T(4,128)S(1)}, f32[4,512]{1,0:T(4,128)S(1)}, u32[]{:S(2)}, u32[]{:S(2)}) %collective-permute-start.18) | collective-permute-done | bytes 8224 | tf_op jit(solution)/shard_map/ppermute | solution.py:151
  54.5 1.7 %collective-permute-start.19 = (f32[4,512]{1,0:T(4,128)S(1)}, f32[4,512]{1,0:T(4,128)S(1)}, u32[]{:S(2)}, u32[]{:S(2)}) collective-permute-start(f32[4,512]{1,0:T(4,128)S(1)} %fusion.55), channel_id=1, source_target_pairs={{0,2},{1,3},{2,0},{3,1},{4,6},{5,7},{6,4},{7,5},{8,10},{9,11},{10,... | collective-permute-start | bytes 24584 | tf_op jit(solution)/shard_map/ppermute | solution.py:151
  56.3 1.2 %bitcast_dynamic-update-slice_fusion.7 = (bf16[4,512,256]{2,1,0:T(8,128)(2,1)S(1)}, bf16[512,256]{1,0:T(8,128)(2,1)S(1)}, f32[512,256]{1,0:T(8,128)}, f32[512,256]{1,0:T(8,128)}) fusion(bf16[4,512,256]{2,1,0:T(8,128)(2,1)S(1)} %broadcast.106.clone.1, s32[]{:T(128)S(6)} %select_n.175, f32[512,256]{1,0:T(8,128)S(1)} %copy-done, ...), kind=kLoop, calls=%fused_computation.87 | loop fusion | flops 1310720 | bytes 3147780 | tf_op jit(solution)/shard_map/jit(dynamic_update_index_in_dim)/dynamic_update_slice | solution.py:28
  57.5 1.5 %collective-permute-start.12 = (bf16[512,256]{1,0:T(8,128)(2,1)S(1)}, bf16[512,256]{1,0:T(8,128)(2,1)S(1)}, u32[]{:S(2)}, u32[]{:S(2)}) collective-permute-start(bf16[512,256]{1,0:T(8,128)(2,1)S(1)} %get-tuple-element.49), channel_id=1, source_target_pairs={{0,16},{8,24},{16,0},{24,8},{1,17},{9,25},{17,1},{25,9},{2,18},{10... | collective-permute-start | bytes 786440 | tf_op jit(solution)/shard_map/ppermute | solution.py:56
  59.1 2.7 %collective-permute-start.20 = (f32[4,512]{1,0:T(4,128)S(1)}, f32[4,512]{1,0:T(4,128)S(1)}, u32[]{:S(2)}, u32[]{:S(2)}) collective-permute-start(f32[4,512]{1,0:T(4,128)S(1)} %fusion.68), channel_id=1, source_target_pairs={{0,4},{1,5},{2,6},{3,7},{4,0},{5,1},{6,2},{7,3},{8,12},{9,13},{10,... | collective-permute-start | bytes 24584 | tf_op jit(solution)/shard_map/ppermute | solution.py:151
  61.8 1.2 %bitcast_dynamic-update-slice_fusion.11 = (bf16[4,512,256]{2,1,0:T(8,128)(2,1)S(1)}, bf16[512,256]{1,0:T(8,128)(2,1)S(1)}, f32[512,256]{1,0:T(8,128)}, f32[512,256]{1,0:T(8,128)}) fusion(bf16[4,512,256]{2,1,0:T(8,128)(2,1)S(1)} %broadcast.106.clone, s32[]{:T(128)S(6)} %select_n.175, f32[512,256]{1,0:T(8,128)S(1)} %copy-done.1, ...), kind=kLoop, calls=%fused_computation.91 | loop fusion | flops 1310720 | bytes 3147780 | tf_op jit(solution)/shard_map/jit(dynamic_update_index_in_dim)/dynamic_update_slice | solution.py:28
  63.0 0.7 collective-permute-start.9
  64.0 1.2 %constant_dynamic-update-slice_fusion.2 = (bf16[256,2048]{1,0:T(8,128)(2,1)S(1)}, bf16[256,512]{1,0:T(8,128)(2,1)S(1)}, f32[256,512]{1,0:T(8,128)}, f32[256,512]{1,0:T(8,128)}) fusion(bf16[256,2048]{1,0:T(8,128)(2,1)S(1)} %broadcast_in_dim.70, s32[]{:T(128)S(6)} %select_n.186, f32[256,512]{1,0:T(8,128)S(1)} %copy-done.2, ...), kind=kLoop, calls=%fused_computation.102 | loop fusion | flops 1310720 | bytes 3147780 | tf_op jit(solution)/shard_map/dynamic_update_slice | solution.py:29
  65.2 0.2 collective-permute-start.24
  65.5 1.2 %bitcast_dynamic-update-slice_fusion.3 = (bf16[4,512,256]{2,1,0:T(8,128)(2,1)S(1)}, bf16[512,256]{1,0:T(8,128)(2,1)S(1)}, f32[512,256]{1,0:T(8,128)}, f32[512,256]{1,0:T(8,128)}) fusion(bf16[4,512,256]{2,1,0:T(8,128)(2,1)S(1)} %broadcast.106.clone.2, s32[]{:T(128)S(6)} %select_n.175, f32[512,256]{1,0:T(8,128)S(1)} %copy-done.3, ...), kind=kLoop, calls=%fused_computation.83 | loop fusion | flops 1310720 | bytes 3147780 | tf_op jit(solution)/shard_map/jit(dynamic_update_index_in_dim)/dynamic_update_slice | solution.py:28
  66.7 1.3 %collective-permute-start.25 = (bf16[256,512]{1,0:T(8,128)(2,1)S(1)}, bf16[256,512]{1,0:T(8,128)(2,1)S(1)}, u32[]{:S(2)}, u32[]{:S(2)}) collective-permute-start(bf16[256,512]{1,0:T(8,128)(2,1)S(1)} %get-tuple-element.37), channel_id=1, source_target_pairs={{0,16},{8,24},{16,0},{24,8},{1,17},{9,25},{17,1},{25,9},{2,18},{10... | collective-permute-start | bytes 786440 | tf_op jit(solution)/shard_map/ppermute | solution.py:56
  68.1 0.8 collective-permute-start.22
  69.0 3.2 %collective-permute-done.9 = bf16[512,256]{1,0:T(8,128)(2,1)S(1)} collective-permute-done((bf16[512,256]{1,0:T(8,128)(2,1)S(1)}, bf16[512,256]{1,0:T(8,128)(2,1)S(1)}, u32[]{:S(2)}, u32[]{:S(2)}) %collective-permute-start.9) | collective-permute-done | bytes 262176 | tf_op jit(solution)/shard_map/ppermute | solution.py:56
  72.2 5.6 %collective-permute-done.25 = bf16[256,512]{1,0:T(8,128)(2,1)S(1)} collective-permute-done((bf16[256,512]{1,0:T(8,128)(2,1)S(1)}, bf16[256,512]{1,0:T(8,128)(2,1)S(1)}, u32[]{:S(2)}, u32[]{:S(2)}) %collective-permute-start.25) | collective-permute-done | bytes 262176 | tf_op jit(solution)/shard_map/ppermute | solution.py:56
  77.8 0.5 collective-permute-start.26
  78.3 4.7 %collective-permute-done.22 = bf16[512,256]{1,0:T(8,128)(2,1)S(1)} collective-permute-done((bf16[512,256]{1,0:T(8,128)(2,1)S(1)}, bf16[512,256]{1,0:T(8,128)(2,1)S(1)}, u32[]{:S(2)}, u32[]{:S(2)}) %collective-permute-start.22) | collective-permute-done | bytes 262176 | tf_op jit(solution)/shard_map/ppermute | solution.py:56
  83.3 1.3 %collective-permute-done.23 = bf16[512,256]{1,0:T(8,128)(2,1)S(1)} collective-permute-done((bf16[512,256]{1,0:T(8,128)(2,1)S(1)}, bf16[512,256]{1,0:T(8,128)(2,1)S(1)}, u32[]{:S(2)}, u32[]{:S(2)}) %collective-permute-start.23) | collective-permute-done | bytes 262176 | tf_op jit(solution)/shard_map/ppermute | solution.py:50
  84.7 0.9 %copy-done.4 = bf16[4,512,256]{2,1,0:T(8,128)(2,1)} copy-done((bf16[4,512,256]{2,1,0:T(8,128)(2,1)}, bf16[4,512,256]{2,1,0:T(8,128)(2,1)S(1)}, u32[]{:S(2)}) %copy-start.4) | copy-done | bytes 1048600
  85.6 0.3 copy-done.5
  (115 shorter events, 2.1 us)
Async XLA Ops:
  0.7 7.6 %copy-start.19 = (f32[512]{0:T(512)S(1)}, f32[512]{0:T(512)}, u32[]{:S(2)}) copy-start(f32[512]{0:T(512)} %param.28) | copy-start | bytes 6148
  0.7 7.6 %copy-start.18 = (f32[512]{0:T(512)S(1)}, f32[512]{0:T(512)}, u32[]{:S(2)}) copy-start(f32[512]{0:T(512)} %param.29) | copy-start | bytes 6148
  0.7 7.6 %copy-start.17 = (f32[512]{0:T(512)S(1)}, f32[512]{0:T(512)}, u32[]{:S(2)}) copy-start(f32[512]{0:T(512)} %param.34) | copy-start | bytes 6148
  0.7 7.6 %copy-start.16 = (f32[512]{0:T(512)S(1)}, f32[512]{0:T(512)}, u32[]{:S(2)}) copy-start(f32[512]{0:T(512)} %param.35) | copy-start | bytes 6148
  0.7 15.4 %copy-start.1 = (f32[512,256]{1,0:T(8,128)S(1)}, f32[512,256]{1,0:T(8,128)}, u32[]{:S(2)}) copy-start(f32[512,256]{1,0:T(8,128)} %param.24) | copy-start | bytes 1572868
  0.7 15.5 %copy-start = (f32[512,256]{1,0:T(8,128)S(1)}, f32[512,256]{1,0:T(8,128)}, u32[]{:S(2)}) copy-start(f32[512,256]{1,0:T(8,128)} %param.25) | copy-start | bytes 1572868
  0.7 15.7 %copy-start.3 = (f32[512,256]{1,0:T(8,128)S(1)}, f32[512,256]{1,0:T(8,128)}, u32[]{:S(2)}) copy-start(f32[512,256]{1,0:T(8,128)} %param.26) | copy-start | bytes 1572868
  0.8 15.8 %copy-start.14 = (f32[1,2048]{1,0:T(1,128)S(1)}, f32[1,2048]{1,0:T(1,128)}, u32[]{:S(2)}) copy-start(f32[1,2048]{1,0:T(1,128)} %param.23) | copy-start | bytes 24580
  0.8 15.8 %copy-start.15 = (f32[1,2048]{1,0:T(1,128)S(1)}, f32[1,2048]{1,0:T(1,128)}, u32[]{:S(2)}) copy-start(f32[1,2048]{1,0:T(1,128)} %param.22) | copy-start | bytes 24580
  0.8 15.8 %copy-start.2 = (f32[256,512]{1,0:T(8,128)S(1)}, f32[256,512]{1,0:T(8,128)}, u32[]{:S(2)}) copy-start(f32[256,512]{1,0:T(8,128)} %param.27) | copy-start | bytes 1572868
  2.0 2.1 %collective-permute-start.1 = (f32[512,256]{1,0:T(8,128)S(1)}, f32[512,256]{1,0:T(8,128)S(1)}, u32[]{:S(2)}, u32[]{:S(2)}) collective-permute-start(f32[512,256]{1,0:T(8,128)S(1)} %dynamic-slice_bitcast_fusion), channel_id=1, source_target_pairs={{0,8},{8,0},{16,24},{24,16},{1,9},{9,1},{17,25},{25,17},{2,10},{10... | collective-permute-start | bytes 1572872 | tf_op jit(solution)/shard_map/ppermute | solution.py:50
  2.6 17.6 %collective-permute-start.3 = (f32[2048,256]{1,0:T(8,128)}, f32[2048,256]{1,0:T(8,128)}, u32[]{:S(2)}, u32[]{:S(2)}) collective-permute-start(f32[2048,256]{1,0:T(8,128)} %bitcast.117), channel_id=1, source_target_pairs={{0,8},{8,0},{16,24},{24,16},{1,9},{9,1},{17,25},{25,17},{2,10},{10... | collective-permute-start | bytes 6291464 | tf_op jit(solution)/shard_map/ppermute | solution.py:50
  5.3 10.1 %collective-permute-start.2 = (bf16[512,256]{1,0:T(8,128)(2,1)S(1)}, bf16[512,256]{1,0:T(8,128)(2,1)S(1)}, u32[]{:S(2)}, u32[]{:S(2)}) collective-permute-start(bf16[512,256]{1,0:T(8,128)(2,1)S(1)} %fusion.18), channel_id=1, source_target_pairs={{0,16},{8,24},{16,0},{24,8},{1,17},{9,25},{17,1},{25,9},{2,18},{10... | collective-permute-start | bytes 786440 | tf_op jit(solution)/shard_map/ppermute | solution.py:56
  8.3 7.1 %collective-permute-start.27 = (f32[6144]{0:T(1024)S(1)}, f32[6144]{0:T(1024)S(1)}, u32[]{:S(2)}, u32[]{:S(2)}) collective-permute-start(f32[6144]{0:T(1024)S(1)} %pad_maximum_fusion), channel_id=1, source_target_pairs={{0,16},{8,24},{16,0},{24,8},{1,17},{9,25},{17,1},{25,9},{2,18},{10... | collective-permute-start | bytes 73736 | tf_op jit(solution)/shard_map/ppermute | solution.py:56
  8.4 21.8 %collective-permute-start = (f32[2048,256]{1,0:T(8,128)}, f32[2048,256]{1,0:T(8,128)}, u32[]{:S(2)}, u32[]{:S(2)}) collective-permute-start(f32[2048,256]{1,0:T(8,128)} %bitcast.112), channel_id=1, source_target_pairs={{0,8},{8,0},{16,24},{24,16},{1,9},{9,1},{17,25},{25,17},{2,10},{10... | collective-permute-start | bytes 6291464 | tf_op jit(solution)/shard_map/ppermute | solution.py:50
  8.5 30.3 %collective-permute-start.16 = (f32[256,2048]{1,0:T(8,128)}, f32[256,2048]{1,0:T(8,128)}, u32[]{:S(2)}, u32[]{:S(2)}) collective-permute-start(f32[256,2048]{1,0:T(8,128)} %bitcast.123), channel_id=1, source_target_pairs={{0,8},{8,0},{16,24},{24,16},{1,9},{9,1},{17,25},{25,17},{2,10},{10... | collective-permute-start | bytes 6291464 | tf_op jit(solution)/shard_map/ppermute | solution.py:50
  15.4 18.9 %collective-permute-start.14 = (f32[2048,256]{1,0:T(8,128)}, f32[2048,256]{1,0:T(8,128)}, u32[]{:S(2)}, u32[]{:S(2)}) collective-permute-start(f32[2048,256]{1,0:T(8,128)} %bitcast.120), channel_id=1, source_target_pairs={{0,8},{8,0},{16,24},{24,16},{1,9},{9,1},{17,25},{25,17},{2,10},{10... | collective-permute-start | bytes 6291464 | tf_op jit(solution)/shard_map/ppermute | solution.py:50
  15.5 4.4 %collective-permute-start.28 = (f32[4,4,512]{2,0,1:T(4,128)S(1)}, f32[4,4,512]{2,0,1:T(4,128)S(1)}, u32[]{:S(2)}, u32[]{:S(2)}) collective-permute-start(f32[4,4,512]{2,0,1:T(4,128)S(1)} %dynamic_update_slice.73), channel_id=1, source_target_pairs={{0,8},{8,0},{16,24},{24,16},{1,9},{9,1},{17,25},{25,17},{2,10},{10... | collective-permute-start | bytes 98312 | tf_op jit(solution)/shard_map/ppermute | solution.py:50
  19.9 3.5 %collective-permute-start.29 = (f32[2,2048]{1,0:T(2,128)S(1)}, f32[2,2048]{1,0:T(2,128)S(1)}, u32[]{:S(2)}, u32[]{:S(2)}) collective-permute-start(f32[2,2048]{1,0:T(2,128)S(1)} %fusion.39), channel_id=1, source_target_pairs={{0,8},{8,0},{16,24},{24,16},{1,9},{9,1},{17,25},{25,17},{2,10},{10... | collective-permute-start | bytes 49160 | tf_op jit(solution)/shard_map/ppermute | solution.py:50
  21.6 12.8 %copy-start.8 = (f32[1,2048,256]{2,1,0:T(8,128)S(1)}, f32[1,2048,256]{2,1,0:T(8,128)}, u32[]{:S(2)}) copy-start(f32[1,2048,256]{2,1,0:T(8,128)} %param.20) | copy-start | bytes 6291460
  21.6 8.6 %collective-permute-start.4 = (bf16[512,256]{1,0:T(8,128)(2,1)S(1)}, bf16[512,256]{1,0:T(8,128)(2,1)S(1)}, u32[]{:S(2)}, u32[]{:S(2)}) collective-permute-start(bf16[512,256]{1,0:T(8,128)(2,1)S(1)} %fusion.22), channel_id=1, source_target_pairs={{0,16},{8,24},{16,0},{24,8},{1,17},{9,25},{17,1},{25,9},{2,18},{10... | collective-permute-start | bytes 786440 | tf_op jit(solution)/shard_map/ppermute | solution.py:56
  30.2 8.6 %copy-start.9 = (f32[1,256,2048]{2,1,0:T(8,128)S(1)}, f32[1,256,2048]{2,1,0:T(8,128)}, u32[]{:S(2)}) copy-start(f32[1,256,2048]{2,1,0:T(8,128)} %param.21) | copy-start | bytes 6291460
  32.5 4.6 %collective-permute-start.5 = (f32[4,512]{1,0:T(4,128)S(1)}, f32[4,512]{1,0:T(4,128)S(1)}, u32[]{:S(2)}, u32[]{:S(2)}) collective-permute-start(f32[4,512]{1,0:T(4,128)S(1)} %pad_maximum_fusion.2), channel_id=1, source_target_pairs={{0,1},{1,0},{2,3},{3,2},{4,5},{5,4},{6,7},{7,6},{8,9},{9,8},{10,11... | collective-permute-start | bytes 24584 | tf_op jit(solution)/shard_map/ppermute | solution.py:151
  35.5 9.2 %collective-permute-start.15 = (bf16[512,256]{1,0:T(8,128)(2,1)S(1)}, bf16[512,256]{1,0:T(8,128)(2,1)S(1)}, u32[]{:S(2)}, u32[]{:S(2)}) collective-permute-start(bf16[512,256]{1,0:T(8,128)(2,1)S(1)} %fusion.28), channel_id=1, source_target_pairs={{0,16},{8,24},{16,0},{24,8},{1,17},{9,25},{17,1},{25,9},{2,18},{10... | collective-permute-start | bytes 786440 | tf_op jit(solution)/shard_map/ppermute | solution.py:56
  37.1 7.6 %collective-permute-start.6 = (f32[4,512]{1,0:T(4,128)S(1)}, f32[4,512]{1,0:T(4,128)S(1)}, u32[]{:S(2)}, u32[]{:S(2)}) collective-permute-start(f32[4,512]{1,0:T(4,128)S(1)} %fusion.56), channel_id=1, source_target_pairs={{0,2},{1,3},{2,0},{3,1},{4,6},{5,7},{6,4},{7,5},{8,10},{9,11},{10,... | collective-permute-start | bytes 24584 | tf_op jit(solution)/shard_map/ppermute | solution.py:151
  40.0 9.4 %collective-permute-start.17 = (bf16[256,512]{1,0:T(8,128)(2,1)S(1)}, bf16[256,512]{1,0:T(8,128)(2,1)S(1)}, u32[]{:S(2)}, u32[]{:S(2)}) collective-permute-start(bf16[256,512]{1,0:T(8,128)(2,1)S(1)} %fusion.32), channel_id=1, source_target_pairs={{0,16},{8,24},{16,0},{24,8},{1,17},{9,25},{17,1},{25,9},{2,18},{10... | collective-permute-start | bytes 786440 | tf_op jit(solution)/shard_map/ppermute | solution.py:56
  44.8 11.5 %copy-start.10 = (f32[512,256]{1,0:T(8,128)S(1)}, f32[512,256]{1,0:T(8,128)}, u32[]{:S(2)}) copy-start(f32[512,256]{1,0:T(8,128)} %param.31) | copy-start | bytes 1572868
  44.8 4.6 %collective-permute-start.7 = (f32[4,512]{1,0:T(4,128)S(1)}, f32[4,512]{1,0:T(4,128)S(1)}, u32[]{:S(2)}, u32[]{:S(2)}) collective-permute-start(f32[4,512]{1,0:T(4,128)S(1)} %fusion.69), channel_id=1, source_target_pairs={{0,4},{1,5},{2,6},{3,7},{4,0},{5,1},{6,2},{7,3},{8,12},{9,13},{10,... | collective-permute-start | bytes 24584 | tf_op jit(solution)/shard_map/ppermute | solution.py:151
  50.8 3.7 %collective-permute-start.18 = (f32[4,512]{1,0:T(4,128)S(1)}, f32[4,512]{1,0:T(4,128)S(1)}, u32[]{:S(2)}, u32[]{:S(2)}) collective-permute-start(f32[4,512]{1,0:T(4,128)S(1)} %pad_maximum_fusion.3), channel_id=1, source_target_pairs={{0,1},{1,0},{2,3},{3,2},{4,5},{5,4},{6,7},{7,6},{8,9},{9,8},{10,11... | collective-permute-start | bytes 24584 | tf_op jit(solution)/shard_map/ppermute | solution.py:151
  54.5 4.5 %collective-permute-start.19 = (f32[4,512]{1,0:T(4,128)S(1)}, f32[4,512]{1,0:T(4,128)S(1)}, u32[]{:S(2)}, u32[]{:S(2)}) collective-permute-start(f32[4,512]{1,0:T(4,128)S(1)} %fusion.55), channel_id=1, source_target_pairs={{0,2},{1,3},{2,0},{3,1},{4,6},{5,7},{6,4},{7,5},{8,10},{9,11},{10,... | collective-permute-start | bytes 24584 | tf_op jit(solution)/shard_map/ppermute | solution.py:151
  56.3 5.5 %copy-start.11 = (f32[512,256]{1,0:T(8,128)S(1)}, f32[512,256]{1,0:T(8,128)}, u32[]{:S(2)}) copy-start(f32[512,256]{1,0:T(8,128)} %param.30) | copy-start | bytes 1572868
  57.5 9.2 %collective-permute-start.11 = (bf16[512,256]{1,0:T(8,128)(2,1)S(1)}, bf16[512,256]{1,0:T(8,128)(2,1)S(1)}, u32[]{:S(2)}, u32[]{:S(2)}) collective-permute-start(bf16[512,256]{1,0:T(8,128)(2,1)S(1)} %get-tuple-element.49), channel_id=1, source_target_pairs={{0,8},{8,0},{16,24},{24,16},{1,9},{9,1},{17,25},{25,17},{2,10},{10... | collective-permute-start | bytes 786440 | tf_op jit(solution)/shard_map/ppermute | solution.py:50
  57.5 10.5 %collective-permute-start.12 = (bf16[512,256]{1,0:T(8,128)(2,1)S(1)}, bf16[512,256]{1,0:T(8,128)(2,1)S(1)}, u32[]{:S(2)}, u32[]{:S(2)}) collective-permute-start(bf16[512,256]{1,0:T(8,128)(2,1)S(1)} %get-tuple-element.49), channel_id=1, source_target_pairs={{0,16},{8,24},{16,0},{24,8},{1,17},{9,25},{17,1},{25,9},{2,18},{10... | collective-permute-start | bytes 786440 | tf_op jit(solution)/shard_map/ppermute | solution.py:56
  59.1 4.7 %collective-permute-start.20 = (f32[4,512]{1,0:T(4,128)S(1)}, f32[4,512]{1,0:T(4,128)S(1)}, u32[]{:S(2)}, u32[]{:S(2)}) collective-permute-start(f32[4,512]{1,0:T(4,128)S(1)} %fusion.68), channel_id=1, source_target_pairs={{0,4},{1,5},{2,6},{3,7},{4,0},{5,1},{6,2},{7,3},{8,12},{9,13},{10,... | collective-permute-start | bytes 24584 | tf_op jit(solution)/shard_map/ppermute | solution.py:151
  61.8 2.1 %copy-start.12 = (f32[256,512]{1,0:T(8,128)S(1)}, f32[256,512]{1,0:T(8,128)}, u32[]{:S(2)}) copy-start(f32[256,512]{1,0:T(8,128)} %param.33) | copy-start | bytes 1572868
  63.0 5.1 %collective-permute-start.8 = (bf16[512,256]{1,0:T(8,128)(2,1)S(1)}, bf16[512,256]{1,0:T(8,128)(2,1)S(1)}, u32[]{:S(2)}, u32[]{:S(2)}) collective-permute-start(bf16[512,256]{1,0:T(8,128)(2,1)S(1)} %get-tuple-element.53), channel_id=1, source_target_pairs={{0,8},{8,0},{16,24},{24,16},{1,9},{9,1},{17,25},{25,17},{2,10},{10... | collective-permute-start | bytes 786440 | tf_op jit(solution)/shard_map/ppermute | solution.py:50
  63.0 9.2 %collective-permute-start.9 = (bf16[512,256]{1,0:T(8,128)(2,1)S(1)}, bf16[512,256]{1,0:T(8,128)(2,1)S(1)}, u32[]{:S(2)}, u32[]{:S(2)}) collective-permute-start(bf16[512,256]{1,0:T(8,128)(2,1)S(1)} %get-tuple-element.53), channel_id=1, source_target_pairs={{0,16},{8,24},{16,0},{24,8},{1,17},{9,25},{17,1},{25,9},{2,18},{10... | collective-permute-start | bytes 786440 | tf_op jit(solution)/shard_map/ppermute | solution.py:56
  63.9 1.5 %copy-start.13 = (f32[512,256]{1,0:T(8,128)S(1)}, f32[512,256]{1,0:T(8,128)}, u32[]{:S(2)}) copy-start(f32[512,256]{1,0:T(8,128)} %param.32) | copy-start | bytes 1572868
  65.2 18.0 %collective-permute-start.24 = (bf16[256,512]{1,0:T(8,128)(2,1)S(1)}, bf16[256,512]{1,0:T(8,128)(2,1)S(1)}, u32[]{:S(2)}, u32[]{:S(2)}) collective-permute-start(bf16[256,512]{1,0:T(8,128)(2,1)S(1)} %get-tuple-element.37), channel_id=1, source_target_pairs={{0,8},{8,0},{16,24},{24,16},{1,9},{9,1},{17,25},{25,17},{2,10},{10... | collective-permute-start | bytes 786440 | tf_op jit(solution)/shard_map/ppermute | solution.py:50
  66.7 11.1 %collective-permute-start.25 = (bf16[256,512]{1,0:T(8,128)(2,1)S(1)}, bf16[256,512]{1,0:T(8,128)(2,1)S(1)}, u32[]{:S(2)}, u32[]{:S(2)}) collective-permute-start(bf16[256,512]{1,0:T(8,128)(2,1)S(1)} %get-tuple-element.37), channel_id=1, source_target_pairs={{0,16},{8,24},{16,0},{24,8},{1,17},{9,25},{17,1},{25,9},{2,18},{10... | collective-permute-start | bytes 786440 | tf_op jit(solution)/shard_map/ppermute | solution.py:56
  68.0 9.8 %collective-permute-start.21 = (bf16[512,256]{1,0:T(8,128)(2,1)S(1)}, bf16[512,256]{1,0:T(8,128)(2,1)S(1)}, u32[]{:S(2)}, u32[]{:S(2)}) collective-permute-start(bf16[512,256]{1,0:T(8,128)(2,1)S(1)} %get-tuple-element.41), channel_id=1, source_target_pairs={{0,8},{8,0},{16,24},{24,16},{1,9},{9,1},{17,25},{25,17},{2,10},{10... | collective-permute-start | bytes 786440 | tf_op jit(solution)/shard_map/ppermute | solution.py:50
  68.1 14.9 %collective-permute-start.22 = (bf16[512,256]{1,0:T(8,128)(2,1)S(1)}, bf16[512,256]{1,0:T(8,128)(2,1)S(1)}, u32[]{:S(2)}, u32[]{:S(2)}) collective-permute-start(bf16[512,256]{1,0:T(8,128)(2,1)S(1)} %get-tuple-element.41), channel_id=1, source_target_pairs={{0,16},{8,24},{16,0},{24,8},{1,17},{9,25},{17,1},{25,9},{2,18},{10... | collective-permute-start | bytes 786440 | tf_op jit(solution)/shard_map/ppermute | solution.py:56
  72.2 11.0 %collective-permute-start.13 = (bf16[512,256]{1,0:T(8,128)(2,1)S(1)}, bf16[512,256]{1,0:T(8,128)(2,1)S(1)}, u32[]{:S(2)}, u32[]{:S(2)}) collective-permute-start(bf16[512,256]{1,0:T(8,128)(2,1)S(1)} %collective-permute-done.12), channel_id=1, source_target_pairs={{0,8},{8,0},{16,24},{24,16},{1,9},{9,1},{17,25},{25,17},{2,10},{10... | collective-permute-start | bytes 786440 | tf_op jit(solution)/shard_map/ppermute | solution.py:50
  77.8 5.5 %collective-permute-start.10 = (bf16[512,256]{1,0:T(8,128)(2,1)S(1)}, bf16[512,256]{1,0:T(8,128)(2,1)S(1)}, u32[]{:S(2)}, u32[]{:S(2)}) collective-permute-start(bf16[512,256]{1,0:T(8,128)(2,1)S(1)} %collective-permute-done.9), channel_id=1, source_target_pairs={{0,8},{8,0},{16,24},{24,16},{1,9},{9,1},{17,25},{25,17},{2,10},{10... | collective-permute-start | bytes 786440 | tf_op jit(solution)/shard_map/ppermute | solution.py:50
  77.8 6.8 %collective-permute-start.26 = (bf16[256,512]{1,0:T(8,128)(2,1)S(1)}, bf16[256,512]{1,0:T(8,128)(2,1)S(1)}, u32[]{:S(2)}, u32[]{:S(2)}) collective-permute-start(bf16[256,512]{1,0:T(8,128)(2,1)S(1)} %collective-permute-done.25), channel_id=1, source_target_pairs={{0,8},{8,0},{16,24},{24,16},{1,9},{9,1},{17,25},{25,17},{2,10},{10... | collective-permute-start | bytes 786440 | tf_op jit(solution)/shard_map/ppermute | solution.py:50
  83.1 1.5 %collective-permute-start.23 = (bf16[512,256]{1,0:T(8,128)(2,1)S(1)}, bf16[512,256]{1,0:T(8,128)(2,1)S(1)}, u32[]{:S(2)}, u32[]{:S(2)}) collective-permute-start(bf16[512,256]{1,0:T(8,128)(2,1)S(1)} %collective-permute-done.22), channel_id=1, source_target_pairs={{0,8},{8,0},{16,24},{24,16},{1,9},{9,1},{17,25},{25,17},{2,10},{10... | collective-permute-start | bytes 786440 | tf_op jit(solution)/shard_map/ppermute | solution.py:50
  83.3 1.4 %copy-start.6 = (bf16[4,512,256]{2,1,0:T(8,128)(2,1)}, bf16[4,512,256]{2,1,0:T(8,128)(2,1)S(1)}, u32[]{:S(2)}) copy-start(bf16[4,512,256]{2,1,0:T(8,128)(2,1)S(1)} %bitcast_dynamic-update-slice_fusion.4) | copy-start | bytes 3145732
  83.3 1.4 %copy-start.7 = (bf16[4,512,256]{2,1,0:T(8,128)(2,1)}, bf16[4,512,256]{2,1,0:T(8,128)(2,1)S(1)}, u32[]{:S(2)}) copy-start(bf16[4,512,256]{2,1,0:T(8,128)(2,1)S(1)} %bitcast_dynamic-update-slice_fusion.8) | copy-start | bytes 3145732
  (2 other events, 2.2 us)

commit v3 on v2

--- a/solution.py
+++ b/solution.py
@@ -146,19 +146,24 @@
     def stages(value):
         if models & (models - 1):
             return [lax.psum(value, "model")]
-        found, bit = [], 1
-        while bit < models:
-            got = lax.ppermute(value, "model", [(i, i ^ bit) for i in range(models)])
-            value = value + got
+        bits = [1 << i for i in range(models.bit_length() - 1)]
+        groups = [bits[:1]] + [bits[i : i + 2] for i in range(1, len(bits), 2)]
+        found = []
+        for group in groups:
+            flips = [*group[::-1], sum(group)] if len(group) > 1 else group
+            total = value
+            for flip in flips:
+                pairs = [(i, i ^ flip) for i in range(models)]
+                total = total + lax.ppermute(value, "model", pairs)
+            value = total
             found.append(value)
-            bit *= 2
         return found
 
     slope_q = reduce_in("query")
     slope_k = reduce_in("key")
     first = stages(jnp.stack([own_size("query"), own_size("key"), slope_q, slope_k]))
     slope_v = reduce_in("value", first[0])
-    slope_m = reduce_in("mixed", first[-1])
+    slope_m = reduce_in("mixed", first[0])
     second = stages(jnp.stack([own_size("value"), own_size("mixed"), slope_v, slope_m]))
     total = first[-1]
     finish("query", total[0], total[2])

time: 86.4 us -> 86.6 us (level)
  starting transfers between devices: 25.1 us -> 27.2 us
  waiting for transfers between devices: 38.4 us -> 36.6 us
    ppermute x6 -> x8, waiting for transfers between devices: 4 us -> 2.06 us  [stages(): total = total + lax.ppermute(value, 'model', pairs)]
    ppermute x6 -> x8, starting transfers between devices: 10.7 us -> 12.4 us  [stages(): total = total + lax.ppermute(value, 'model', pairs)]
  transfers between devices with their start and end apart: 30 -> 32, of which waited for: 11 -> 12; matrix products, arithmetic and copies ran while one was open for 20% -> 18% of each run, Pallas kernels for 0% -> 0%
where the time goes in v3:
time: 86.6 us; the launch traced here: 86.1 us
  waiting for transfers between devices  36.6 us (42%)
  starting transfers between devices  27.2 us (31%)
  other arithmetic  16.4 us (19%)
  local copies, waits for them, and re-layouts  4.64 us (5%)
  between operations  1.37 us (2%)
    ppermute x9, waiting for transfers between devices, to_chip(): return lax.ppermute(value, 'replica', pairs)  29.3 us
    ppermute x8, starting transfers between devices, stages(): total = total + lax.ppermute(value, 'model', pairs)  12.4 us
    ppermute x9, starting transfers between devices, to_chip(): return lax.ppermute(value, 'replica', pairs)  12.1 us
    ppermute x15, waiting for transfers between devices, to_pair(): return lax.ppermute(value, 'replica', [(i, i ^ 1) for i in range(count)])  5.24 us
    convert_element_type x4, other arithmetic, encode(): return jnp.where(value < 0, -size, size).astype(jnp.bfloat16)  5.02 us
    reduce_sum x3, other arithmetic, reduce_in(): return jnp.sum(mean[n] * mean[n], axis=1 - axis_of[n])  4.9 us
    dynamic_update_slice x3, other arithmetic, put_block(): lax.dynamic_update_index_in_dim(split, block[None], index, axis=0)  3.67 us
    ppermute x15, starting transfers between devices, to_pair(): return lax.ppermute(value, 'replica', [(i, i ^ 1) for i in range(count)])  2.64 us
  transfers between devices with their start and end apart: 32, of which 12 were waited for; matrix products, arithmetic and copies ran while one was open for 18% of the time, Pallas kernels for 0%

profile of v3, /device:TPU:0, one launch (start us, length us, event | category | flops | bytes accessed | tf_op | source)
XLA Modules:
  0.0 86.1 jit_solution(7452282489033271118)
XLA Ops:
  0.8 1.2 %dynamic-slice_bitcast_fusion = f32[512,256]{1,0:T(8,128)S(1)} fusion(f32[4,512,256]{2,1,0:T(8,128)} %bitcast.110, s32[]{:T(128)S(6)} %select_n.170), kind=kLoop, calls=%fused_computation.79 | loop fusion | bytes 1048580 | tf_op jit(solution)/shard_map/jit(dynamic_index_in_dim)/squeeze | solution.py:20
  2.0 0.6 collective-permute-start.1
  2.7 0.7 fusion.40
  3.4 0.7 collective-permute-done.1
  4.1 1.2 %fusion.18 = bf16[512,256]{1,0:T(8,128)(2,1)S(1)} fusion(f32[512,256]{1,0:T(8,128)S(1)} %collective-permute-done.1, f32[4,512,256]{2,1,0:T(8,128)} %bitcast.111, s32[]{:T(128)S(6)} %select_n.169), kind=kLoop, calls=%fused_computation.42 | loop fusion | flops 1310720 | bytes 1310724 | tf_op jit(solution)/shard_map/convert_element_type | solution.py:65
  5.3 2.9 %collective-permute-start.2 = (bf16[512,256]{1,0:T(8,128)(2,1)S(1)}, bf16[512,256]{1,0:T(8,128)(2,1)S(1)}, u32[]{:S(2)}, u32[]{:S(2)}) collective-permute-start(bf16[512,256]{1,0:T(8,128)(2,1)S(1)} %fusion.18), channel_id=1, source_target_pairs={{0,16},{8,24},{16,0},{24,8},{1,17},{9,25},{17,1},{25,9},{2,18},{10... | collective-permute-start | bytes 786440 | tf_op jit(solution)/shard_map/ppermute | solution.py:56
  8.5 0.5 collective-permute-start.17
  9.2 6.3 %collective-permute-done.29 = f32[6144]{0:T(1024)S(1)} collective-permute-done((f32[6144]{0:T(1024)S(1)}, f32[6144]{0:T(1024)S(1)}, u32[]{:S(2)}, u32[]{:S(2)}) %collective-permute-start.29) | collective-permute-done | bytes 24608 | tf_op jit(solution)/shard_map/ppermute | solution.py:56
  15.5 0.6 collective-permute-start.30
  16.7 3.2 %collective-permute-done.30 = f32[4,4,512]{2,0,1:T(4,128)S(1)} collective-permute-done((f32[4,4,512]{2,0,1:T(4,128)S(1)}, f32[4,4,512]{2,0,1:T(4,128)S(1)}, u32[]{:S(2)}, u32[]{:S(2)}) %collective-permute-start.30) | collective-permute-done | bytes 32800 | tf_op jit(solution)/shard_map/ppermute | solution.py:50
  20.2 1.2 %fusion.22 = bf16[512,256]{1,0:T(8,128)(2,1)S(1)} fusion(f32[4,512,256]{2,1,0:T(8,128)} %bitcast.11, s32[]{:T(128)S(6)} %select_n.169, f32[4,512,256]{2,1,0:T(8,128)S(1)} %bitcast.118), kind=kLoop, calls=%fused_computation.46 | loop fusion | flops 1310720 | bytes 1310724 | tf_op jit(solution)/shard_map/convert_element_type | solution.py:65
  21.4 1.8 %collective-permute-start.4 = (bf16[512,256]{1,0:T(8,128)(2,1)S(1)}, bf16[512,256]{1,0:T(8,128)(2,1)S(1)}, u32[]{:S(2)}, u32[]{:S(2)}) collective-permute-start(bf16[512,256]{1,0:T(8,128)(2,1)S(1)} %fusion.22), channel_id=1, source_target_pairs={{0,16},{8,24},{16,0},{24,8},{1,17},{9,25},{17,1},{25,9},{2,18},{10... | collective-permute-start | bytes 786440 | tf_op jit(solution)/shard_map/ppermute | solution.py:56
  23.3 1.4 %fusion.32 = bf16[256,512]{1,0:T(8,128)(2,1)S(1)} fusion(f32[256,2048]{1,0:T(8,128)} %collective-permute-done.17, s32[]{:T(128)S(6)} %select_n.183, f32[1,256,2048]{2,1,0:T(8,128)} %param.21), kind=kLoop, calls=%fused_computation.56 | loop fusion | flops 1310720 | bytes 1310724 | tf_op jit(solution)/shard_map/convert_element_type | solution.py:65
  24.7 0.4 collective-permute-start.18
  25.0 1.2 %fusion.28 = bf16[512,256]{1,0:T(8,128)(2,1)S(1)} fusion(f32[4,512,256]{2,1,0:T(8,128)} %bitcast.29, s32[]{:T(128)S(6)} %select_n.169, f32[4,512,256]{2,1,0:T(8,128)S(1)} %bitcast.121), kind=kLoop, calls=%fused_computation.52 | loop fusion | flops 1310720 | bytes 1310724 | tf_op jit(solution)/shard_map/convert_element_type | solution.py:65
  26.2 1.8 %collective-permute-start.16 = (bf16[512,256]{1,0:T(8,128)(2,1)S(1)}, bf16[512,256]{1,0:T(8,128)(2,1)S(1)}, u32[]{:S(2)}, u32[]{:S(2)}) collective-permute-start(bf16[512,256]{1,0:T(8,128)(2,1)S(1)} %fusion.28), channel_id=1, source_target_pairs={{0,16},{8,24},{16,0},{24,8},{1,17},{9,25},{17,1},{25,9},{2,18},{10... | collective-permute-start | bytes 786440 | tf_op jit(solution)/shard_map/ppermute | solution.py:56
  28.0 2.6 %collective-permute-done.4 = bf16[512,256]{1,0:T(8,128)(2,1)S(1)} collective-permute-done((bf16[512,256]{1,0:T(8,128)(2,1)S(1)}, bf16[512,256]{1,0:T(8,128)(2,1)S(1)}, u32[]{:S(2)}, u32[]{:S(2)}) %collective-permute-start.4) | collective-permute-done | bytes 262176 | tf_op jit(solution)/shard_map/ppermute | solution.py:56
  30.7 2.0 %multiply_reduce_fusion.4 = (f32[512]{0:T(512)S(1)}, f32[512,256]{1,0:T(8,128)S(1)}, f32[512]{0:T(512)S(1)}, f32[512,256]{1,0:T(8,128)S(1)}) fusion(bf16[512,256]{1,0:T(8,128)(2,1)S(1)} %collective-permute-done.4, f32[4,512,256]{2,1,0:T(8,128)} %bitcast.11, s32[]{:T(128)S(6)} %select_n.167, f32[4,512,256]{2,1,0:T(8,128)S(1)} %bitcast.119, ...), kind=kLoop, calls=%fused_computation.75 | loop fusion | flops 3144704 | bytes 3674116 | tf_op jit(solution)/shard_map/reduce_sum | solution.py:119
  32.7 1.8 %collective-permute-start.5 = (f32[4,512]{1,0:T(4,128)S(1)}, f32[4,512]{1,0:T(4,128)S(1)}, u32[]{:S(2)}, u32[]{:S(2)}) collective-permute-start(f32[4,512]{1,0:T(4,128)S(1)} %pad_maximum_fusion.2), channel_id=1, source_target_pairs={{0,1},{1,0},{2,3},{3,2},{4,5},{5,4},{6,7},{7,6},{8,9},{9,8},{10,11... | collective-permute-start | bytes 24584 | tf_op jit(solution)/shard_map/ppermute | solution.py:157
  34.4 0.6 slice_reduce_fusion
  35.1 1.3 %collective-permute-done.5 = f32[4,512]{1,0:T(4,128)S(1)} collective-permute-done((f32[4,512]{1,0:T(4,128)S(1)}, f32[4,512]{1,0:T(4,128)S(1)}, u32[]{:S(2)}, u32[]{:S(2)}) %collective-permute-start.5) | collective-permute-done | bytes 8224 | tf_op jit(solution)/shard_map/ppermute | solution.py:157
  36.4 4.9 %collective-permute-done.16 = bf16[512,256]{1,0:T(8,128)(2,1)S(1)} collective-permute-done((bf16[512,256]{1,0:T(8,128)(2,1)S(1)}, bf16[512,256]{1,0:T(8,128)(2,1)S(1)}, u32[]{:S(2)}, u32[]{:S(2)}) %collective-permute-start.16) | collective-permute-done | bytes 262176 | tf_op jit(solution)/shard_map/ppermute | solution.py:56
  41.3 1.4 %multiply_reduce_fusion.1 = (f32[512]{0:T(512)S(1)}, f32[512,256]{1,0:T(8,128)S(1)}) fusion(bf16[512,256]{1,0:T(8,128)(2,1)S(1)} %collective-permute-done.16, f32[4,512,256]{2,1,0:T(8,128)} %bitcast.29, s32[]{:T(128)S(6)} %select_n.167, f32[4,512,256]{2,1,0:T(8,128)S(1)} %bitcast.122), kind=kLoop, calls=%fused_computation.70 | loop fusion | flops 1572352 | bytes 1837060 | tf_op jit(solution)/shard_map/reduce_sum | solution.py:119
  42.7 1.5 %multiply_reduce_fusion = (f32[512]{0:T(512)S(1)}, f32[256,512]{1,0:T(8,128)S(1)}) fusion(bf16[256,512]{1,0:T(8,128)(2,1)S(1)} %collective-permute-done.18, f32[256,2048]{1,0:T(8,128)} %collective-permute-done.17, s32[]{:T(128)S(6)} %select_n.182, f32[1,256,2048]{2,1,0:T(8,128)} %param.21), kind=kLoop, calls=%fused_computation.69 | loop fusion | flops 1572352 | bytes 1837060 | tf_op jit(solution)/shard_map/reduce_sum | solution.py:119
  44.2 1.8 %collective-permute-start.19 = (f32[4,512]{1,0:T(4,128)S(1)}, f32[4,512]{1,0:T(4,128)S(1)}, u32[]{:S(2)}, u32[]{:S(2)}) collective-permute-start(f32[4,512]{1,0:T(4,128)S(1)} %pad_maximum_fusion.3), channel_id=1, source_target_pairs={{0,1},{1,0},{2,3},{3,2},{4,5},{5,4},{6,7},{7,6},{8,9},{9,8},{10,11... | collective-permute-start | bytes 24584 | tf_op jit(solution)/shard_map/ppermute | solution.py:157
  46.0 0.7 fusion.66
  46.7 2.6 %collective-permute-start.6 = (f32[4,512]{1,0:T(4,128)S(1)}, f32[4,512]{1,0:T(4,128)S(1)}, u32[]{:S(2)}, u32[]{:S(2)}) collective-permute-start(f32[4,512]{1,0:T(4,128)S(1)} %fusion.56), channel_id=1, source_target_pairs={{0,4},{1,5},{2,6},{3,7},{4,0},{5,1},{6,2},{7,3},{8,12},{9,13},{10,... | collective-permute-start | bytes 24584 | tf_op jit(solution)/shard_map/ppermute | solution.py:157
  49.2 1.6 %collective-permute-start.7 = (f32[4,512]{1,0:T(4,128)S(1)}, f32[4,512]{1,0:T(4,128)S(1)}, u32[]{:S(2)}, u32[]{:S(2)}) collective-permute-start(f32[4,512]{1,0:T(4,128)S(1)} %fusion.56), channel_id=1, source_target_pairs={{0,2},{1,3},{2,0},{3,1},{4,6},{5,7},{6,4},{7,5},{8,10},{9,11},{10,... | collective-permute-start | bytes 24584 | tf_op jit(solution)/shard_map/ppermute | solution.py:157
  51.1 1.8 %collective-permute-start.20 = (f32[4,512]{1,0:T(4,128)S(1)}, f32[4,512]{1,0:T(4,128)S(1)}, u32[]{:S(2)}, u32[]{:S(2)}) collective-permute-start(f32[4,512]{1,0:T(4,128)S(1)} %fusion.55), channel_id=1, source_target_pairs={{0,4},{1,5},{2,6},{3,7},{4,0},{5,1},{6,2},{7,3},{8,12},{9,13},{10,... | collective-permute-start | bytes 24584 | tf_op jit(solution)/shard_map/ppermute | solution.py:157
  52.8 2.5 %collective-permute-start.21 = (f32[4,512]{1,0:T(4,128)S(1)}, f32[4,512]{1,0:T(4,128)S(1)}, u32[]{:S(2)}, u32[]{:S(2)}) collective-permute-start(f32[4,512]{1,0:T(4,128)S(1)} %fusion.55), channel_id=1, source_target_pairs={{0,2},{1,3},{2,0},{3,1},{4,6},{5,7},{6,4},{7,5},{8,10},{9,11},{10,... | collective-permute-start | bytes 24584 | tf_op jit(solution)/shard_map/ppermute | solution.py:157
  55.5 0.7 collective-permute-done.8
  56.4 1.2 %bitcast_dynamic-update-slice_fusion.7 = (bf16[4,512,256]{2,1,0:T(8,128)(2,1)S(1)}, bf16[512,256]{1,0:T(8,128)(2,1)S(1)}, f32[512,256]{1,0:T(8,128)}, f32[512,256]{1,0:T(8,128)}) fusion(bf16[4,512,256]{2,1,0:T(8,128)(2,1)S(1)} %broadcast.106.clone.1, s32[]{:T(128)S(6)} %select_n.175, f32[512,256]{1,0:T(8,128)S(1)} %copy-done, ...), kind=kLoop, calls=%fused_computation.87 | loop fusion | flops 1310720 | bytes 3147780 | tf_op jit(solution)/shard_map/jit(dynamic_update_index_in_dim)/dynamic_update_slice | solution.py:28
  57.7 1.5 %collective-permute-start.13 = (bf16[512,256]{1,0:T(8,128)(2,1)S(1)}, bf16[512,256]{1,0:T(8,128)(2,1)S(1)}, u32[]{:S(2)}, u32[]{:S(2)}) collective-permute-start(bf16[512,256]{1,0:T(8,128)(2,1)S(1)} %get-tuple-element.49), channel_id=1, source_target_pairs={{0,16},{8,24},{16,0},{24,8},{1,17},{9,25},{17,1},{25,9},{2,18},{10... | collective-permute-start | bytes 786440 | tf_op jit(solution)/shard_map/ppermute | solution.py:56
  59.3 1.2 %bitcast_dynamic-update-slice_fusion.11 = (bf16[4,512,256]{2,1,0:T(8,128)(2,1)S(1)}, bf16[512,256]{1,0:T(8,128)(2,1)S(1)}, f32[512,256]{1,0:T(8,128)}, f32[512,256]{1,0:T(8,128)}) fusion(bf16[4,512,256]{2,1,0:T(8,128)(2,1)S(1)} %broadcast.106.clone, s32[]{:T(128)S(6)} %select_n.175, f32[512,256]{1,0:T(8,128)S(1)} %copy-done.1, ...), kind=kLoop, calls=%fused_computation.91 | loop fusion | flops 1310720 | bytes 3147780 | tf_op jit(solution)/shard_map/jit(dynamic_update_index_in_dim)/dynamic_update_slice | solution.py:28
  60.5 0.2 collective-permute-start.9
  60.7 0.5 collective-permute-start.10
  61.4 1.2 %constant_dynamic-update-slice_fusion.2 = (bf16[256,2048]{1,0:T(8,128)(2,1)S(1)}, bf16[256,512]{1,0:T(8,128)(2,1)S(1)}, f32[256,512]{1,0:T(8,128)}, f32[256,512]{1,0:T(8,128)}) fusion(bf16[256,2048]{1,0:T(8,128)(2,1)S(1)} %broadcast_in_dim.70, s32[]{:T(128)S(6)} %select_n.186, f32[256,512]{1,0:T(8,128)S(1)} %copy-done.2, ...), kind=kLoop, calls=%fused_computation.102 | loop fusion | flops 1310720 | bytes 3147780 | tf_op jit(solution)/shard_map/dynamic_update_slice | solution.py:29
  62.7 1.2 %bitcast_dynamic-update-slice_fusion.3 = (bf16[4,512,256]{2,1,0:T(8,128)(2,1)S(1)}, bf16[512,256]{1,0:T(8,128)(2,1)S(1)}, f32[512,256]{1,0:T(8,128)}, f32[512,256]{1,0:T(8,128)}) fusion(bf16[4,512,256]{2,1,0:T(8,128)(2,1)S(1)} %broadcast.106.clone.2, s32[]{:T(128)S(6)} %select_n.175, f32[512,256]{1,0:T(8,128)S(1)} %copy-done.3, ...), kind=kLoop, calls=%fused_computation.83 | loop fusion | flops 1310720 | bytes 3147780 | tf_op jit(solution)/shard_map/jit(dynamic_update_index_in_dim)/dynamic_update_slice | solution.py:28
  64.0 1.5 %collective-permute-start.27 = (bf16[256,512]{1,0:T(8,128)(2,1)S(1)}, bf16[256,512]{1,0:T(8,128)(2,1)S(1)}, u32[]{:S(2)}, u32[]{:S(2)}) collective-permute-start(bf16[256,512]{1,0:T(8,128)(2,1)S(1)} %get-tuple-element.37), channel_id=1, source_target_pairs={{0,16},{8,24},{16,0},{24,8},{1,17},{9,25},{17,1},{25,9},{2,18},{10... | collective-permute-start | bytes 786440 | tf_op jit(solution)/shard_map/ppermute | solution.py:56
  65.5 1.3 %collective-permute-done.13 = bf16[512,256]{1,0:T(8,128)(2,1)S(1)} collective-permute-done((bf16[512,256]{1,0:T(8,128)(2,1)S(1)}, bf16[512,256]{1,0:T(8,128)(2,1)S(1)}, u32[]{:S(2)}, u32[]{:S(2)}) %collective-permute-start.13) | collective-permute-done | bytes 262176 | tf_op jit(solution)/shard_map/ppermute | solution.py:56
  66.9 1.6 %collective-permute-start.24 = (bf16[512,256]{1,0:T(8,128)(2,1)S(1)}, bf16[512,256]{1,0:T(8,128)(2,1)S(1)}, u32[]{:S(2)}, u32[]{:S(2)}) collective-permute-start(bf16[512,256]{1,0:T(8,128)(2,1)S(1)} %get-tuple-element.41), channel_id=1, source_target_pairs={{0,16},{8,24},{16,0},{24,8},{1,17},{9,25},{17,1},{25,9},{2,18},{10... | collective-permute-start | bytes 786440 | tf_op jit(solution)/shard_map/ppermute | solution.py:56
  68.5 4.0 %collective-permute-done.10 = bf16[512,256]{1,0:T(8,128)(2,1)S(1)} collective-permute-done((bf16[512,256]{1,0:T(8,128)(2,1)S(1)}, bf16[512,256]{1,0:T(8,128)(2,1)S(1)}, u32[]{:S(2)}, u32[]{:S(2)}) %collective-permute-start.10) | collective-permute-done | bytes 262176 | tf_op jit(solution)/shard_map/ppermute | solution.py:56
  72.5 5.6 %collective-permute-done.27 = bf16[256,512]{1,0:T(8,128)(2,1)S(1)} collective-permute-done((bf16[256,512]{1,0:T(8,128)(2,1)S(1)}, bf16[256,512]{1,0:T(8,128)(2,1)S(1)}, u32[]{:S(2)}, u32[]{:S(2)}) %collective-permute-start.27) | collective-permute-done | bytes 262176 | tf_op jit(solution)/shard_map/ppermute | solution.py:56
  78.1 0.5 collective-permute-start.28
  78.6 4.6 %collective-permute-done.24 = bf16[512,256]{1,0:T(8,128)(2,1)S(1)} collective-permute-done((bf16[512,256]{1,0:T(8,128)(2,1)S(1)}, bf16[512,256]{1,0:T(8,128)(2,1)S(1)}, u32[]{:S(2)}, u32[]{:S(2)}) %collective-permute-start.24) | collective-permute-done | bytes 262176 | tf_op jit(solution)/shard_map/ppermute | solution.py:56
  83.5 1.3 %collective-permute-done.25 = bf16[512,256]{1,0:T(8,128)(2,1)S(1)} collective-permute-done((bf16[512,256]{1,0:T(8,128)(2,1)S(1)}, bf16[512,256]{1,0:T(8,128)(2,1)S(1)}, u32[]{:S(2)}, u32[]{:S(2)}) %collective-permute-start.25) | collective-permute-done | bytes 262176 | tf_op jit(solution)/shard_map/ppermute | solution.py:50
  84.9 0.9 %copy-done.4 = bf16[4,512,256]{2,1,0:T(8,128)(2,1)} copy-done((bf16[4,512,256]{2,1,0:T(8,128)(2,1)}, bf16[4,512,256]{2,1,0:T(8,128)(2,1)S(1)}, u32[]{:S(2)}) %copy-start.4) | copy-done | bytes 1048600
  85.8 0.3 copy-done.5
  (117 shorter events, 2.6 us)
Async XLA Ops:
  0.7 7.6 %copy-start.19 = (f32[512]{0:T(512)S(1)}, f32[512]{0:T(512)}, u32[]{:S(2)}) copy-start(f32[512]{0:T(512)} %param.28) | copy-start | bytes 6148
  0.7 7.6 %copy-start.18 = (f32[512]{0:T(512)S(1)}, f32[512]{0:T(512)}, u32[]{:S(2)}) copy-start(f32[512]{0:T(512)} %param.29) | copy-start | bytes 6148
  0.7 7.6 %copy-start.17 = (f32[512]{0:T(512)S(1)}, f32[512]{0:T(512)}, u32[]{:S(2)}) copy-start(f32[512]{0:T(512)} %param.34) | copy-start | bytes 6148
  0.7 7.6 %copy-start.16 = (f32[512]{0:T(512)S(1)}, f32[512]{0:T(512)}, u32[]{:S(2)}) copy-start(f32[512]{0:T(512)} %param.35) | copy-start | bytes 6148
  0.7 15.4 %copy-start.1 = (f32[512,256]{1,0:T(8,128)S(1)}, f32[512,256]{1,0:T(8,128)}, u32[]{:S(2)}) copy-start(f32[512,256]{1,0:T(8,128)} %param.24) | copy-start | bytes 1572868
  0.7 15.5 %copy-start = (f32[512,256]{1,0:T(8,128)S(1)}, f32[512,256]{1,0:T(8,128)}, u32[]{:S(2)}) copy-start(f32[512,256]{1,0:T(8,128)} %param.25) | copy-start | bytes 1572868
  0.7 15.7 %copy-start.3 = (f32[512,256]{1,0:T(8,128)S(1)}, f32[512,256]{1,0:T(8,128)}, u32[]{:S(2)}) copy-start(f32[512,256]{1,0:T(8,128)} %param.26) | copy-start | bytes 1572868
  0.8 15.8 %copy-start.14 = (f32[1,2048]{1,0:T(1,128)S(1)}, f32[1,2048]{1,0:T(1,128)}, u32[]{:S(2)}) copy-start(f32[1,2048]{1,0:T(1,128)} %param.23) | copy-start | bytes 24580
  0.8 15.8 %copy-start.15 = (f32[1,2048]{1,0:T(1,128)S(1)}, f32[1,2048]{1,0:T(1,128)}, u32[]{:S(2)}) copy-start(f32[1,2048]{1,0:T(1,128)} %param.22) | copy-start | bytes 24580
  0.8 15.8 %copy-start.2 = (f32[256,512]{1,0:T(8,128)S(1)}, f32[256,512]{1,0:T(8,128)}, u32[]{:S(2)}) copy-start(f32[256,512]{1,0:T(8,128)} %param.27) | copy-start | bytes 1572868
  2.0 2.1 %collective-permute-start.1 = (f32[512,256]{1,0:T(8,128)S(1)}, f32[512,256]{1,0:T(8,128)S(1)}, u32[]{:S(2)}, u32[]{:S(2)}) collective-permute-start(f32[512,256]{1,0:T(8,128)S(1)} %dynamic-slice_bitcast_fusion), channel_id=1, source_target_pairs={{0,8},{8,0},{16,24},{24,16},{1,9},{9,1},{17,25},{25,17},{2,10},{10... | collective-permute-start | bytes 1572872 | tf_op jit(solution)/shard_map/ppermute | solution.py:50
  2.6 17.6 %collective-permute-start.3 = (f32[2048,256]{1,0:T(8,128)}, f32[2048,256]{1,0:T(8,128)}, u32[]{:S(2)}, u32[]{:S(2)}) collective-permute-start(f32[2048,256]{1,0:T(8,128)} %bitcast.117), channel_id=1, source_target_pairs={{0,8},{8,0},{16,24},{24,16},{1,9},{9,1},{17,25},{25,17},{2,10},{10... | collective-permute-start | bytes 6291464 | tf_op jit(solution)/shard_map/ppermute | solution.py:50
  5.3 10.1 %collective-permute-start.2 = (bf16[512,256]{1,0:T(8,128)(2,1)S(1)}, bf16[512,256]{1,0:T(8,128)(2,1)S(1)}, u32[]{:S(2)}, u32[]{:S(2)}) collective-permute-start(bf16[512,256]{1,0:T(8,128)(2,1)S(1)} %fusion.18), channel_id=1, source_target_pairs={{0,16},{8,24},{16,0},{24,8},{1,17},{9,25},{17,1},{25,9},{2,18},{10... | collective-permute-start | bytes 786440 | tf_op jit(solution)/shard_map/ppermute | solution.py:56
  8.3 7.1 %collective-permute-start.29 = (f32[6144]{0:T(1024)S(1)}, f32[6144]{0:T(1024)S(1)}, u32[]{:S(2)}, u32[]{:S(2)}) collective-permute-start(f32[6144]{0:T(1024)S(1)} %pad_maximum_fusion), channel_id=1, source_target_pairs={{0,16},{8,24},{16,0},{24,8},{1,17},{9,25},{17,1},{25,9},{2,18},{10... | collective-permute-start | bytes 73736 | tf_op jit(solution)/shard_map/ppermute | solution.py:56
  8.4 22.2 %collective-permute-start = (f32[2048,256]{1,0:T(8,128)}, f32[2048,256]{1,0:T(8,128)}, u32[]{:S(2)}, u32[]{:S(2)}) collective-permute-start(f32[2048,256]{1,0:T(8,128)} %bitcast.112), channel_id=1, source_target_pairs={{0,8},{8,0},{16,24},{24,16},{1,9},{9,1},{17,25},{25,17},{2,10},{10... | collective-permute-start | bytes 6291464 | tf_op jit(solution)/shard_map/ppermute | solution.py:50
  8.5 14.8 %collective-permute-start.17 = (f32[256,2048]{1,0:T(8,128)}, f32[256,2048]{1,0:T(8,128)}, u32[]{:S(2)}, u32[]{:S(2)}) collective-permute-start(f32[256,2048]{1,0:T(8,128)} %bitcast.123), channel_id=1, source_target_pairs={{0,8},{8,0},{16,24},{24,16},{1,9},{9,1},{17,25},{25,17},{2,10},{10... | collective-permute-start | bytes 6291464 | tf_op jit(solution)/shard_map/ppermute | solution.py:50
  15.4 9.6 %collective-permute-start.15 = (f32[2048,256]{1,0:T(8,128)}, f32[2048,256]{1,0:T(8,128)}, u32[]{:S(2)}, u32[]{:S(2)}) collective-permute-start(f32[2048,256]{1,0:T(8,128)} %bitcast.120), channel_id=1, source_target_pairs={{0,8},{8,0},{16,24},{24,16},{1,9},{9,1},{17,25},{25,17},{2,10},{10... | collective-permute-start | bytes 6291464 | tf_op jit(solution)/shard_map/ppermute | solution.py:50
  15.5 4.4 %collective-permute-start.30 = (f32[4,4,512]{2,0,1:T(4,128)S(1)}, f32[4,4,512]{2,0,1:T(4,128)S(1)}, u32[]{:S(2)}, u32[]{:S(2)}) collective-permute-start(f32[4,4,512]{2,0,1:T(4,128)S(1)} %dynamic_update_slice.73), channel_id=1, source_target_pairs={{0,8},{8,0},{16,24},{24,16},{1,9},{9,1},{17,25},{25,17},{2,10},{10... | collective-permute-start | bytes 98312 | tf_op jit(solution)/shard_map/ppermute | solution.py:50
  16.1 4.1 %copy-start.8 = (f32[1,2048,256]{2,1,0:T(8,128)S(1)}, f32[1,2048,256]{2,1,0:T(8,128)}, u32[]{:S(2)}) copy-start(f32[1,2048,256]{2,1,0:T(8,128)} %param.19) | copy-start | bytes 6291460
  16.4 8.6 %copy-start.9 = (f32[1,2048,256]{2,1,0:T(8,128)S(1)}, f32[1,2048,256]{2,1,0:T(8,128)}, u32[]{:S(2)}) copy-start(f32[1,2048,256]{2,1,0:T(8,128)} %param.20) | copy-start | bytes 6291460
  19.9 3.3 %collective-permute-start.31 = (f32[2,2048]{1,0:T(2,128)S(1)}, f32[2,2048]{1,0:T(2,128)S(1)}, u32[]{:S(2)}, u32[]{:S(2)}) collective-permute-start(f32[2,2048]{1,0:T(2,128)S(1)} %fusion.39), channel_id=1, source_target_pairs={{0,8},{8,0},{16,24},{24,16},{1,9},{9,1},{17,25},{25,17},{2,10},{10... | collective-permute-start | bytes 49160 | tf_op jit(solution)/shard_map/ppermute | solution.py:50
  21.4 9.2 %collective-permute-start.4 = (bf16[512,256]{1,0:T(8,128)(2,1)S(1)}, bf16[512,256]{1,0:T(8,128)(2,1)S(1)}, u32[]{:S(2)}, u32[]{:S(2)}) collective-permute-start(bf16[512,256]{1,0:T(8,128)(2,1)S(1)} %fusion.22), channel_id=1, source_target_pairs={{0,16},{8,24},{16,0},{24,8},{1,17},{9,25},{17,1},{25,9},{2,18},{10... | collective-permute-start | bytes 786440 | tf_op jit(solution)/shard_map/ppermute | solution.py:56
  24.7 11.8 %collective-permute-start.18 = (bf16[256,512]{1,0:T(8,128)(2,1)S(1)}, bf16[256,512]{1,0:T(8,128)(2,1)S(1)}, u32[]{:S(2)}, u32[]{:S(2)}) collective-permute-start(bf16[256,512]{1,0:T(8,128)(2,1)S(1)} %fusion.32), channel_id=1, source_target_pairs={{0,16},{8,24},{16,0},{24,8},{1,17},{9,25},{17,1},{25,9},{2,18},{10... | collective-permute-start | bytes 786440 | tf_op jit(solution)/shard_map/ppermute | solution.py:56
  26.2 15.1 %collective-permute-start.16 = (bf16[512,256]{1,0:T(8,128)(2,1)S(1)}, bf16[512,256]{1,0:T(8,128)(2,1)S(1)}, u32[]{:S(2)}, u32[]{:S(2)}) collective-permute-start(bf16[512,256]{1,0:T(8,128)(2,1)S(1)} %fusion.28), channel_id=1, source_target_pairs={{0,16},{8,24},{16,0},{24,8},{1,17},{9,25},{17,1},{25,9},{2,18},{10... | collective-permute-start | bytes 786440 | tf_op jit(solution)/shard_map/ppermute | solution.py:56
  32.7 3.7 %collective-permute-start.5 = (f32[4,512]{1,0:T(4,128)S(1)}, f32[4,512]{1,0:T(4,128)S(1)}, u32[]{:S(2)}, u32[]{:S(2)}) collective-permute-start(f32[4,512]{1,0:T(4,128)S(1)} %pad_maximum_fusion.2), channel_id=1, source_target_pairs={{0,1},{1,0},{2,3},{3,2},{4,5},{5,4},{6,7},{7,6},{8,9},{9,8},{10,11... | collective-permute-start | bytes 24584 | tf_op jit(solution)/shard_map/ppermute | solution.py:157
  36.4 20.0 %copy-start.10 = (f32[512,256]{1,0:T(8,128)S(1)}, f32[512,256]{1,0:T(8,128)}, u32[]{:S(2)}) copy-start(f32[512,256]{1,0:T(8,128)} %param.31) | copy-start | bytes 1572868
  44.2 6.8 %collective-permute-start.19 = (f32[4,512]{1,0:T(4,128)S(1)}, f32[4,512]{1,0:T(4,128)S(1)}, u32[]{:S(2)}, u32[]{:S(2)}) collective-permute-start(f32[4,512]{1,0:T(4,128)S(1)} %pad_maximum_fusion.3), channel_id=1, source_target_pairs={{0,1},{1,0},{2,3},{3,2},{4,5},{5,4},{6,7},{7,6},{8,9},{9,8},{10,11... | collective-permute-start | bytes 24584 | tf_op jit(solution)/shard_map/ppermute | solution.py:157
  46.7 8.6 %collective-permute-start.6 = (f32[4,512]{1,0:T(4,128)S(1)}, f32[4,512]{1,0:T(4,128)S(1)}, u32[]{:S(2)}, u32[]{:S(2)}) collective-permute-start(f32[4,512]{1,0:T(4,128)S(1)} %fusion.56), channel_id=1, source_target_pairs={{0,4},{1,5},{2,6},{3,7},{4,0},{5,1},{6,2},{7,3},{8,12},{9,13},{10,... | collective-permute-start | bytes 24584 | tf_op jit(solution)/shard_map/ppermute | solution.py:157
  49.2 6.3 %collective-permute-start.7 = (f32[4,512]{1,0:T(4,128)S(1)}, f32[4,512]{1,0:T(4,128)S(1)}, u32[]{:S(2)}, u32[]{:S(2)}) collective-permute-start(f32[4,512]{1,0:T(4,128)S(1)} %fusion.56), channel_id=1, source_target_pairs={{0,2},{1,3},{2,0},{3,1},{4,6},{5,7},{6,4},{7,5},{8,10},{9,11},{10,... | collective-permute-start | bytes 24584 | tf_op jit(solution)/shard_map/ppermute | solution.py:157
  50.8 5.4 %collective-permute-start.8 = (f32[4,512]{1,0:T(4,128)S(1)}, f32[4,512]{1,0:T(4,128)S(1)}, u32[]{:S(2)}, u32[]{:S(2)}) collective-permute-start(f32[4,512]{1,0:T(4,128)S(1)} %fusion.56), channel_id=1, source_target_pairs={{0,6},{1,7},{2,4},{3,5},{4,2},{5,3},{6,0},{7,1},{8,14},{9,15},{10,... | collective-permute-start | bytes 24584 | tf_op jit(solution)/shard_map/ppermute | solution.py:157
  51.1 9.4 %collective-permute-start.20 = (f32[4,512]{1,0:T(4,128)S(1)}, f32[4,512]{1,0:T(4,128)S(1)}, u32[]{:S(2)}, u32[]{:S(2)}) collective-permute-start(f32[4,512]{1,0:T(4,128)S(1)} %fusion.55), channel_id=1, source_target_pairs={{0,4},{1,5},{2,6},{3,7},{4,0},{5,1},{6,2},{7,3},{8,12},{9,13},{10,... | collective-permute-start | bytes 24584 | tf_op jit(solution)/shard_map/ppermute | solution.py:157
  52.8 7.9 %collective-permute-start.21 = (f32[4,512]{1,0:T(4,128)S(1)}, f32[4,512]{1,0:T(4,128)S(1)}, u32[]{:S(2)}, u32[]{:S(2)}) collective-permute-start(f32[4,512]{1,0:T(4,128)S(1)} %fusion.55), channel_id=1, source_target_pairs={{0,2},{1,3},{2,0},{3,1},{4,6},{5,7},{6,4},{7,5},{8,10},{9,11},{10,... | collective-permute-start | bytes 24584 | tf_op jit(solution)/shard_map/ppermute | solution.py:157
  55.3 5.9 %collective-permute-start.22 = (f32[4,512]{1,0:T(4,128)S(1)}, f32[4,512]{1,0:T(4,128)S(1)}, u32[]{:S(2)}, u32[]{:S(2)}) collective-permute-start(f32[4,512]{1,0:T(4,128)S(1)} %fusion.55), channel_id=1, source_target_pairs={{0,6},{1,7},{2,4},{3,5},{4,2},{5,3},{6,0},{7,1},{8,14},{9,15},{10,... | collective-permute-start | bytes 24584 | tf_op jit(solution)/shard_map/ppermute | solution.py:157
  56.4 2.8 %copy-start.11 = (f32[512,256]{1,0:T(8,128)S(1)}, f32[512,256]{1,0:T(8,128)}, u32[]{:S(2)}) copy-start(f32[512,256]{1,0:T(8,128)} %param.30) | copy-start | bytes 1572868
  57.6 6.3 %collective-permute-start.12 = (bf16[512,256]{1,0:T(8,128)(2,1)S(1)}, bf16[512,256]{1,0:T(8,128)(2,1)S(1)}, u32[]{:S(2)}, u32[]{:S(2)}) collective-permute-start(bf16[512,256]{1,0:T(8,128)(2,1)S(1)} %get-tuple-element.49), channel_id=1, source_target_pairs={{0,8},{8,0},{16,24},{24,16},{1,9},{9,1},{17,25},{25,17},{2,10},{10... | collective-permute-start | bytes 786440 | tf_op jit(solution)/shard_map/ppermute | solution.py:50
  57.7 9.2 %collective-permute-start.13 = (bf16[512,256]{1,0:T(8,128)(2,1)S(1)}, bf16[512,256]{1,0:T(8,128)(2,1)S(1)}, u32[]{:S(2)}, u32[]{:S(2)}) collective-permute-start(bf16[512,256]{1,0:T(8,128)(2,1)S(1)} %get-tuple-element.49), channel_id=1, source_target_pairs={{0,16},{8,24},{16,0},{24,8},{1,17},{9,25},{17,1},{25,9},{2,18},{10... | collective-permute-start | bytes 786440 | tf_op jit(solution)/shard_map/ppermute | solution.py:56
  59.3 2.2 %copy-start.12 = (f32[256,512]{1,0:T(8,128)S(1)}, f32[256,512]{1,0:T(8,128)}, u32[]{:S(2)}) copy-start(f32[256,512]{1,0:T(8,128)} %param.33) | copy-start | bytes 1572868
  60.5 6.4 %collective-permute-start.9 = (bf16[512,256]{1,0:T(8,128)(2,1)S(1)}, bf16[512,256]{1,0:T(8,128)(2,1)S(1)}, u32[]{:S(2)}, u32[]{:S(2)}) collective-permute-start(bf16[512,256]{1,0:T(8,128)(2,1)S(1)} %get-tuple-element.53), channel_id=1, source_target_pairs={{0,8},{8,0},{16,24},{24,16},{1,9},{9,1},{17,25},{25,17},{2,10},{10... | collective-permute-start | bytes 786440 | tf_op jit(solution)/shard_map/ppermute | solution.py:50
  60.7 11.7 %collective-permute-start.10 = (bf16[512,256]{1,0:T(8,128)(2,1)S(1)}, bf16[512,256]{1,0:T(8,128)(2,1)S(1)}, u32[]{:S(2)}, u32[]{:S(2)}) collective-permute-start(bf16[512,256]{1,0:T(8,128)(2,1)S(1)} %get-tuple-element.53), channel_id=1, source_target_pairs={{0,16},{8,24},{16,0},{24,8},{1,17},{9,25},{17,1},{25,9},{2,18},{10... | collective-permute-start | bytes 786440 | tf_op jit(solution)/shard_map/ppermute | solution.py:56
  62.6 20.7 %collective-permute-start.26 = (bf16[256,512]{1,0:T(8,128)(2,1)S(1)}, bf16[256,512]{1,0:T(8,128)(2,1)S(1)}, u32[]{:S(2)}, u32[]{:S(2)}) collective-permute-start(bf16[256,512]{1,0:T(8,128)(2,1)S(1)} %get-tuple-element.37), channel_id=1, source_target_pairs={{0,8},{8,0},{16,24},{24,16},{1,9},{9,1},{17,25},{25,17},{2,10},{10... | collective-permute-start | bytes 786440 | tf_op jit(solution)/shard_map/ppermute | solution.py:50
  64.0 14.1 %collective-permute-start.27 = (bf16[256,512]{1,0:T(8,128)(2,1)S(1)}, bf16[256,512]{1,0:T(8,128)(2,1)S(1)}, u32[]{:S(2)}, u32[]{:S(2)}) collective-permute-start(bf16[256,512]{1,0:T(8,128)(2,1)S(1)} %get-tuple-element.37), channel_id=1, source_target_pairs={{0,16},{8,24},{16,0},{24,8},{1,17},{9,25},{17,1},{25,9},{2,18},{10... | collective-permute-start | bytes 786440 | tf_op jit(solution)/shard_map/ppermute | solution.py:56
  66.8 11.2 %collective-permute-start.23 = (bf16[512,256]{1,0:T(8,128)(2,1)S(1)}, bf16[512,256]{1,0:T(8,128)(2,1)S(1)}, u32[]{:S(2)}, u32[]{:S(2)}) collective-permute-start(bf16[512,256]{1,0:T(8,128)(2,1)S(1)} %get-tuple-element.41), channel_id=1, source_target_pairs={{0,8},{8,0},{16,24},{24,16},{1,9},{9,1},{17,25},{25,17},{2,10},{10... | collective-permute-start | bytes 786440 | tf_op jit(solution)/shard_map/ppermute | solution.py:50
  66.9 16.4 %collective-permute-start.24 = (bf16[512,256]{1,0:T(8,128)(2,1)S(1)}, bf16[512,256]{1,0:T(8,128)(2,1)S(1)}, u32[]{:S(2)}, u32[]{:S(2)}) collective-permute-start(bf16[512,256]{1,0:T(8,128)(2,1)S(1)} %get-tuple-element.41), channel_id=1, source_target_pairs={{0,16},{8,24},{16,0},{24,8},{1,17},{9,25},{17,1},{25,9},{2,18},{10... | collective-permute-start | bytes 786440 | tf_op jit(solution)/shard_map/ppermute | solution.py:56
  72.5 10.9 %collective-permute-start.14 = (bf16[512,256]{1,0:T(8,128)(2,1)S(1)}, bf16[512,256]{1,0:T(8,128)(2,1)S(1)}, u32[]{:S(2)}, u32[]{:S(2)}) collective-permute-start(bf16[512,256]{1,0:T(8,128)(2,1)S(1)} %collective-permute-done.13), channel_id=1, source_target_pairs={{0,8},{8,0},{16,24},{24,16},{1,9},{9,1},{17,25},{25,17},{2,10},{10... | collective-permute-start | bytes 786440 | tf_op jit(solution)/shard_map/ppermute | solution.py:50
  78.1 5.4 %collective-permute-start.11 = (bf16[512,256]{1,0:T(8,128)(2,1)S(1)}, bf16[512,256]{1,0:T(8,128)(2,1)S(1)}, u32[]{:S(2)}, u32[]{:S(2)}) collective-permute-start(bf16[512,256]{1,0:T(8,128)(2,1)S(1)} %collective-permute-done.10), channel_id=1, source_target_pairs={{0,8},{8,0},{16,24},{24,16},{1,9},{9,1},{17,25},{25,17},{2,10},{10... | collective-permute-start | bytes 786440 | tf_op jit(solution)/shard_map/ppermute | solution.py:50
  78.1 6.7 %collective-permute-start.28 = (bf16[256,512]{1,0:T(8,128)(2,1)S(1)}, bf16[256,512]{1,0:T(8,128)(2,1)S(1)}, u32[]{:S(2)}, u32[]{:S(2)}) collective-permute-start(bf16[256,512]{1,0:T(8,128)(2,1)S(1)} %collective-permute-done.27), channel_id=1, source_target_pairs={{0,8},{8,0},{16,24},{24,16},{1,9},{9,1},{17,25},{25,17},{2,10},{10... | collective-permute-start | bytes 786440 | tf_op jit(solution)/shard_map/ppermute | solution.py:50
  83.2 1.5 %collective-permute-start.25 = (bf16[512,256]{1,0:T(8,128)(2,1)S(1)}, bf16[512,256]{1,0:T(8,128)(2,1)S(1)}, u32[]{:S(2)}, u32[]{:S(2)}) collective-permute-start(bf16[512,256]{1,0:T(8,128)(2,1)S(1)} %collective-permute-done.24), channel_id=1, source_target_pairs={{0,8},{8,0},{16,24},{24,16},{1,9},{9,1},{17,25},{25,17},{2,10},{10... | collective-permute-start | bytes 786440 | tf_op jit(solution)/shard_map/ppermute | solution.py:50
  83.4 1.4 %copy-start.6 = (bf16[4,512,256]{2,1,0:T(8,128)(2,1)}, bf16[4,512,256]{2,1,0:T(8,128)(2,1)S(1)}, u32[]{:S(2)}) copy-start(bf16[4,512,256]{2,1,0:T(8,128)(2,1)S(1)} %bitcast_dynamic-update-slice_fusion.4) | copy-start | bytes 3145732
  (4 other events, 4.9 us)
